TPU v7x, 32 devices: a whole 2x2x4 slice. The times are simulated.
32 devices in a mesh: rep: 2 (over y), shard: 16 (over z, x, core).
Axes of the slice: x: 2, y: 2, z: 4, core: 2. Of those that a mesh axis runs over, the one named last changes fastest.
Arguments:
- row_ids: int32 [2, 16, 16, 128], P('rep', 'shard'), may hold values from -1 to 163839, as said below
- grad_rows: bfloat16 [2, 16, 16, 128, 128], P('rep', 'shard'), may hold values from -6 to 6
- touched: int32 [16, 20], P('shard'), may hold values from 0 to 39, as said below
- block_home: int32 [640], replicated, may hold values from 0 to 639, as said below
- embed_table: float32 [163840, 128], P('shard'), may hold values from -4 to 4
- row_accum: float32 [163840], P('shard'), may hold values from 0.001 to 0.1
Outputs:
- new_table: float32 [163840, 128], P('shard')
- new_accum: float32 [163840], P('shard')
Inputs may be any that keep to these rules, and one draw needn't show every extreme that they name: block_home is a permutation of 0 to 639. Each row of touched holds 20 different local block numbers. `row_ids`: A live slot in bucket d of any device names a logical row whose stored row lies on index d of shard, in a local block listed in row d of touched; about three quarters of the slots are live.
All inputs are finite; a program needn't handle non-finite values.
Results may differ from a plain program's by a relative error of at most 0.0003.
Values may be sent and summed in bfloat16 or wider, within the bound.
No kernel may reach another device: no remote copies, remote signals or barrier semaphores. Data moves between devices by JAX's collectives and lax.ppermute only.
A program may use at most 64 MiB of HBM per device.

v0:
```python
import math

import jax
import jax.numpy as jnp
from jax import lax
from jax.sharding import PartitionSpec as P

BLOCK = 256


CLIP_RMS = 0.25
LEARN_RATE = 0.1
DECAY_RATE = 0.05


def block_sums(slot_keys, gradients, touch_count):
    offsets = lax.broadcasted_iota(jnp.int32, (BLOCK, 1), 0)

    def single_block(slot_index):
        onehot = (slot_keys[None, :] == slot_index * BLOCK + offsets).astype(jnp.bfloat16)
        return jnp.dot(onehot, gradients, preferred_element_type=jnp.float32)

    return lax.map(single_block, jnp.arange(touch_count, dtype=jnp.int32))


def adagrad(old_rows, old_accum, gradient):
    next_accum = old_accum + jnp.mean(gradient * gradient, axis=-1)
    next_rows = (
        old_rows * (1.0 - DECAY_RATE) - LEARN_RATE * gradient / jnp.sqrt(next_accum)[..., None]
    )
    return (next_rows, next_accum)


def slot_blocks(recv_ids, recv_grads, block_home, listed, blocks_here, feature_width):
    sample_ids = recv_ids.reshape(-1)
    gradients = recv_grads.reshape(-1, feature_width)
    is_live = sample_ids >= 0
    safe_ids = jnp.where(is_live, sample_ids, 0)
    local_block = block_home[safe_ids // BLOCK] % blocks_here
    touch_count = listed.shape[0]
    matches = local_block[:, None] == listed[None, :]
    positions = jnp.arange(touch_count, dtype=jnp.int32)[None, :]
    slot_index = jnp.sum(jnp.where(matches, positions, 0), axis=1)
    located = jnp.any(matches, axis=1) & is_live
    slot_keys = jnp.where(located, slot_index * BLOCK + safe_ids % BLOCK, -1)
    return block_sums(slot_keys, gradients, touch_count)


def body(row_ids, grad_rows, touched, block_home, embed_table, row_accum):
    feature_width = grad_rows.shape[-1]
    recv_ids, recv_grads = (
        lax.all_to_all(row_ids, "shard", split_axis=2, concat_axis=2, tiled=True),
        lax.all_to_all(grad_rows, "shard", split_axis=2, concat_axis=2, tiled=True),
    )
    recv_ids, recv_grads = (
        lax.all_gather(recv_ids, "rep", axis=0, tiled=True),
        lax.all_gather(recv_grads, "rep", axis=0, tiled=True),
    )
    blocks_here = embed_table.shape[0] // BLOCK
    listed = touched[0]
    touch_count = listed.shape[0]
    blocks = slot_blocks(recv_ids, recv_grads, block_home, listed, blocks_here, feature_width)
    table_blocks = embed_table.reshape(blocks_here, BLOCK, feature_width)
    accum_blocks = row_accum.reshape(blocks_here, BLOCK)
    entries = lax.axis_size("shard") * touch_count * BLOCK * feature_width
    clip_limit = CLIP_RMS * math.sqrt(entries)
    old_rows = table_blocks[listed]
    old_accum = accum_blocks[listed]
    square_sum = lax.psum(jnp.sum(blocks * blocks), "shard")
    clip_factor = clip_limit / jnp.maximum(jnp.sqrt(square_sum), clip_limit)
    new_rows, new_accum = adagrad(old_rows, old_accum, blocks * clip_factor)
    table_out = table_blocks.at[listed].set(new_rows).reshape(-1, feature_width)
    accum_out = accum_blocks.at[listed].set(new_accum).reshape(-1)
    return (table_out, accum_out)


def solution(mesh):
    in_specs = (
        P("rep", "shard", None, None),
        P("rep", "shard", None, None, None),
        P("shard", None),
        P(),
        P("shard", None),
        P("shard"),
    )
    out_specs = (P("shard", None), P("shard"))
    return jax.shard_map(body, mesh=mesh, in_specs=in_specs, out_specs=out_specs, check_vma=False)
```

profile of v0, /device:TPU:0, one launch (start us, length us, event | category | flops | bytes accessed | tf_op | source)
XLA Modules:
  0.0 192.4 jit_solution(3963022375854497573)
XLA Ops:
  7.2 0.0 copy-start
  7.2 4.3 %copy.28 = f32[10240,128]{1,0:T(8,128)} copy(f32[10240,128]{1,0:T(8,128)} %param.12) | data formatting | bytes 10485760
  11.5 13.6 %all_to_all.10 = s32[1,1,16,128]{3,1,0,2:T(1,128)S(1)} all-to-all(s32[1,1,16,128]{3,1,0,2:T(1,128)S(1)} %bitcast.44), channel_id=1, replica_groups=mesh['rep'=2,'shard'=16] {'shard'}, dimensions={2} | all-to-all | bytes 16384 | tf_op jit(solution)/shard_map/all_to_all | solution.py:52
  25.1 3.6 %all-to-all-start.1 = ((bf16[1,1,16,128,128]{4,3,1,0,2:T(8,128)(2,1)}), bf16[1,1,16,128,128]{4,3,1,0,2:T(8,128)(2,1)S(1)}, u32[]{:S(2)}, u32[]{:S(2)}) async-start(bf16[1,1,16,128,128]{4,3,1,0,2:T(8,128)(2,1)} %bitcast.9), calls=%async_computation.1 | async-start | bytes 1048576 | tf_op jit(solution)/shard_map/all_to_all | solution.py:53
  28.7 0.0 all-gather.2.cloned.1.call-start
  28.8 0.6 gather_fusion.2
  29.4 4.4 %all_gather.6 = s32[2,1,16,128]{3,2,1,0:T(8,128)S(1)} all-gather(s32[1,1,16,128]{3,2,1,0:T(8,128)S(1)} %bitcast.43), channel_id=1, replica_groups=mesh['rep'=2,'shard'=16] {'rep'}, dimensions={0}, use_global_device_ids=true | all-gather | bytes 24576 | tf_op jit(solution)/shard_map/all_gather | solution.py:56
  33.8 9.2 %all-to-all-done.1 = bf16[1,1,16,128,128]{4,3,1,0,2:T(8,128)(2,1)S(1)} async-done(((bf16[1,1,16,128,128]{4,3,1,0,2:T(8,128)(2,1)}), bf16[1,1,16,128,128]{4,3,1,0,2:T(8,128)(2,1)S(1)}, u32[]{:S(2)}, u32[]{:S(2)}) %all-to-all-start.1) | async-done | bytes 524320 | tf_op jit(solution)/shard_map/all_to_all | solution.py:53
  42.9 0.8 copy-done.1
  43.8 0.0 all-gather.2.cloned.1.call-update
  43.8 0.1 compare_select_fusion.1
  43.9 16.7 %gather_fusion.1 = s32[4096]{0:T(1024)S(1)} fusion(s32[640]{0:T(1024)S(1)} %copy-done, s32[4096]{0:T(1024)S(1)} %broadcast_clamp_fusion), kind=kCustom, calls=%fused_computation.1 | custom fusion | bytes 49152 | tf_op jit(solution)/shard_map/gather | solution.py:39
  60.6 0.1 compare_reduce_fusion
  60.8 0.1 fusion.12
  60.9 3.8 %all-gather.2.cloned.1.call-done = bf16[2,1,16,128,128]{4,3,2,1,0:T(8,128)(2,1)} async-done(((bf16[1,1,16,128,128]{4,3,2,1,0:T(8,128)(2,1)}), bf16[2,1,16,128,128]{4,3,2,1,0:T(8,128)(2,1)}) %all-gather.2.cloned.1.call-update) | async-done | bytes 1048592 | tf_op jit(solution)/shard_map/all_gather | solution.py:57
  64.7 67.6 %while.11 = (s32[]{:T(128)}, f32[20,256,128]{2,1,0:T(8,128)S(1)}, s32[4096]{0:T(1024)S(1)}, s32[20]{0:T(128)S(1)}, bf16[4096,128]{1,0:T(8,128)(2,1)}, /*index=5*/s32[]{:T(128)}, s32[1]{0:T(128)}) while((s32[]{:T(128)}, f32[20,256,128]{2,1,0:T(8,128)S(1)}, s32[4096]{0:T(1024)S(1)}, s32[20]{0:T(128)S(1)}, ...), condition=%wide.region_3.4_spmd.clone, body=%wide.region_2.3_spmd.clone.sunk | while | flops 269484288 | bytes 1198197 | solution.py:23
  64.7 0.7 dynamic_slice.6
  66.1 2.0 %fusion.25 = f32[20,256,128]{2,1,0:T(8,128)S(1)} fusion(f32[20,256,128]{2,1,0:T(8,128)S(1)} %get-tuple-element.96, s32[]{:T(128)S(6)} %copy.20, bf16[4096,128]{1,0:T(8,128)(2,1)} %get-tuple-element.106, s32[4096]{0:T(1024)S(1)} %get-tuple-element.104, s32[256]{0:T(256)S(1)} %bitcast.48), kind=kOutput, calls=%fused_computation.11.clone.1 | convolution fusion | flops 269484032 | bytes 1197060 | tf_op jit(solution)/shard_map/while/body/eval_jaxpr/dot_general | solution.py:21
  68.1 0.7 dynamic_slice.6
  69.4 2.0 %fusion.25 = f32[20,256,128]{2,1,0:T(8,128)S(1)} fusion(f32[20,256,128]{2,1,0:T(8,128)S(1)} %get-tuple-element.96, s32[]{:T(128)S(6)} %copy.20, bf16[4096,128]{1,0:T(8,128)(2,1)} %get-tuple-element.106, s32[4096]{0:T(1024)S(1)} %get-tuple-element.104, s32[256]{0:T(256)S(1)} %bitcast.48), kind=kOutput, calls=%fused_computation.11.clone.1 | convolution fusion | flops 269484032 | bytes 1197060 | tf_op jit(solution)/shard_map/while/body/eval_jaxpr/dot_general | solution.py:21
  71.4 0.7 dynamic_slice.6
  72.8 2.0 %fusion.25 = f32[20,256,128]{2,1,0:T(8,128)S(1)} fusion(f32[20,256,128]{2,1,0:T(8,128)S(1)} %get-tuple-element.96, s32[]{:T(128)S(6)} %copy.20, bf16[4096,128]{1,0:T(8,128)(2,1)} %get-tuple-element.106, s32[4096]{0:T(1024)S(1)} %get-tuple-element.104, s32[256]{0:T(256)S(1)} %bitcast.48), kind=kOutput, calls=%fused_computation.11.clone.1 | convolution fusion | flops 269484032 | bytes 1197060 | tf_op jit(solution)/shard_map/while/body/eval_jaxpr/dot_general | solution.py:21
  74.8 0.7 dynamic_slice.6
  76.2 2.0 %fusion.25 = f32[20,256,128]{2,1,0:T(8,128)S(1)} fusion(f32[20,256,128]{2,1,0:T(8,128)S(1)} %get-tuple-element.96, s32[]{:T(128)S(6)} %copy.20, bf16[4096,128]{1,0:T(8,128)(2,1)} %get-tuple-element.106, s32[4096]{0:T(1024)S(1)} %get-tuple-element.104, s32[256]{0:T(256)S(1)} %bitcast.48), kind=kOutput, calls=%fused_computation.11.clone.1 | convolution fusion | flops 269484032 | bytes 1197060 | tf_op jit(solution)/shard_map/while/body/eval_jaxpr/dot_general | solution.py:21
  78.2 0.7 dynamic_slice.6
  79.6 2.0 %fusion.25 = f32[20,256,128]{2,1,0:T(8,128)S(1)} fusion(f32[20,256,128]{2,1,0:T(8,128)S(1)} %get-tuple-element.96, s32[]{:T(128)S(6)} %copy.20, bf16[4096,128]{1,0:T(8,128)(2,1)} %get-tuple-element.106, s32[4096]{0:T(1024)S(1)} %get-tuple-element.104, s32[256]{0:T(256)S(1)} %bitcast.48), kind=kOutput, calls=%fused_computation.11.clone.1 | convolution fusion | flops 269484032 | bytes 1197060 | tf_op jit(solution)/shard_map/while/body/eval_jaxpr/dot_general | solution.py:21
  81.6 0.7 dynamic_slice.6
  83.0 2.0 %fusion.25 = f32[20,256,128]{2,1,0:T(8,128)S(1)} fusion(f32[20,256,128]{2,1,0:T(8,128)S(1)} %get-tuple-element.96, s32[]{:T(128)S(6)} %copy.20, bf16[4096,128]{1,0:T(8,128)(2,1)} %get-tuple-element.106, s32[4096]{0:T(1024)S(1)} %get-tuple-element.104, s32[256]{0:T(256)S(1)} %bitcast.48), kind=kOutput, calls=%fused_computation.11.clone.1 | convolution fusion | flops 269484032 | bytes 1197060 | tf_op jit(solution)/shard_map/while/body/eval_jaxpr/dot_general | solution.py:21
  85.0 0.7 dynamic_slice.6
  86.3 2.0 %fusion.25 = f32[20,256,128]{2,1,0:T(8,128)S(1)} fusion(f32[20,256,128]{2,1,0:T(8,128)S(1)} %get-tuple-element.96, s32[]{:T(128)S(6)} %copy.20, bf16[4096,128]{1,0:T(8,128)(2,1)} %get-tuple-element.106, s32[4096]{0:T(1024)S(1)} %get-tuple-element.104, s32[256]{0:T(256)S(1)} %bitcast.48), kind=kOutput, calls=%fused_computation.11.clone.1 | convolution fusion | flops 269484032 | bytes 1197060 | tf_op jit(solution)/shard_map/while/body/eval_jaxpr/dot_general | solution.py:21
  88.3 0.7 dynamic_slice.6
  89.7 2.0 %fusion.25 = f32[20,256,128]{2,1,0:T(8,128)S(1)} fusion(f32[20,256,128]{2,1,0:T(8,128)S(1)} %get-tuple-element.96, s32[]{:T(128)S(6)} %copy.20, bf16[4096,128]{1,0:T(8,128)(2,1)} %get-tuple-element.106, s32[4096]{0:T(1024)S(1)} %get-tuple-element.104, s32[256]{0:T(256)S(1)} %bitcast.48), kind=kOutput, calls=%fused_computation.11.clone.1 | convolution fusion | flops 269484032 | bytes 1197060 | tf_op jit(solution)/shard_map/while/body/eval_jaxpr/dot_general | solution.py:21
  91.7 0.7 dynamic_slice.6
  93.1 2.0 %fusion.25 = f32[20,256,128]{2,1,0:T(8,128)S(1)} fusion(f32[20,256,128]{2,1,0:T(8,128)S(1)} %get-tuple-element.96, s32[]{:T(128)S(6)} %copy.20, bf16[4096,128]{1,0:T(8,128)(2,1)} %get-tuple-element.106, s32[4096]{0:T(1024)S(1)} %get-tuple-element.104, s32[256]{0:T(256)S(1)} %bitcast.48), kind=kOutput, calls=%fused_computation.11.clone.1 | convolution fusion | flops 269484032 | bytes 1197060 | tf_op jit(solution)/shard_map/while/body/eval_jaxpr/dot_general | solution.py:21
  95.1 0.7 dynamic_slice.6
  96.5 2.0 %fusion.25 = f32[20,256,128]{2,1,0:T(8,128)S(1)} fusion(f32[20,256,128]{2,1,0:T(8,128)S(1)} %get-tuple-element.96, s32[]{:T(128)S(6)} %copy.20, bf16[4096,128]{1,0:T(8,128)(2,1)} %get-tuple-element.106, s32[4096]{0:T(1024)S(1)} %get-tuple-element.104, s32[256]{0:T(256)S(1)} %bitcast.48), kind=kOutput, calls=%fused_computation.11.clone.1 | convolution fusion | flops 269484032 | bytes 1197060 | tf_op jit(solution)/shard_map/while/body/eval_jaxpr/dot_general | solution.py:21
  98.5 0.7 dynamic_slice.6
  99.8 2.0 %fusion.25 = f32[20,256,128]{2,1,0:T(8,128)S(1)} fusion(f32[20,256,128]{2,1,0:T(8,128)S(1)} %get-tuple-element.96, s32[]{:T(128)S(6)} %copy.20, bf16[4096,128]{1,0:T(8,128)(2,1)} %get-tuple-element.106, s32[4096]{0:T(1024)S(1)} %get-tuple-element.104, s32[256]{0:T(256)S(1)} %bitcast.48), kind=kOutput, calls=%fused_computation.11.clone.1 | convolution fusion | flops 269484032 | bytes 1197060 | tf_op jit(solution)/shard_map/while/body/eval_jaxpr/dot_general | solution.py:21
  101.9 0.7 dynamic_slice.6
  103.2 2.0 %fusion.25 = f32[20,256,128]{2,1,0:T(8,128)S(1)} fusion(f32[20,256,128]{2,1,0:T(8,128)S(1)} %get-tuple-element.96, s32[]{:T(128)S(6)} %copy.20, bf16[4096,128]{1,0:T(8,128)(2,1)} %get-tuple-element.106, s32[4096]{0:T(1024)S(1)} %get-tuple-element.104, s32[256]{0:T(256)S(1)} %bitcast.48), kind=kOutput, calls=%fused_computation.11.clone.1 | convolution fusion | flops 269484032 | bytes 1197060 | tf_op jit(solution)/shard_map/while/body/eval_jaxpr/dot_general | solution.py:21
  105.2 0.7 dynamic_slice.6
  106.6 2.0 %fusion.25 = f32[20,256,128]{2,1,0:T(8,128)S(1)} fusion(f32[20,256,128]{2,1,0:T(8,128)S(1)} %get-tuple-element.96, s32[]{:T(128)S(6)} %copy.20, bf16[4096,128]{1,0:T(8,128)(2,1)} %get-tuple-element.106, s32[4096]{0:T(1024)S(1)} %get-tuple-element.104, s32[256]{0:T(256)S(1)} %bitcast.48), kind=kOutput, calls=%fused_computation.11.clone.1 | convolution fusion | flops 269484032 | bytes 1197060 | tf_op jit(solution)/shard_map/while/body/eval_jaxpr/dot_general | solution.py:21
  108.6 0.7 dynamic_slice.6
  110.0 2.0 %fusion.25 = f32[20,256,128]{2,1,0:T(8,128)S(1)} fusion(f32[20,256,128]{2,1,0:T(8,128)S(1)} %get-tuple-element.96, s32[]{:T(128)S(6)} %copy.20, bf16[4096,128]{1,0:T(8,128)(2,1)} %get-tuple-element.106, s32[4096]{0:T(1024)S(1)} %get-tuple-element.104, s32[256]{0:T(256)S(1)} %bitcast.48), kind=kOutput, calls=%fused_computation.11.clone.1 | convolution fusion | flops 269484032 | bytes 1197060 | tf_op jit(solution)/shard_map/while/body/eval_jaxpr/dot_general | solution.py:21
  112.0 0.7 dynamic_slice.6
  113.4 2.0 %fusion.25 = f32[20,256,128]{2,1,0:T(8,128)S(1)} fusion(f32[20,256,128]{2,1,0:T(8,128)S(1)} %get-tuple-element.96, s32[]{:T(128)S(6)} %copy.20, bf16[4096,128]{1,0:T(8,128)(2,1)} %get-tuple-element.106, s32[4096]{0:T(1024)S(1)} %get-tuple-element.104, s32[256]{0:T(256)S(1)} %bitcast.48), kind=kOutput, calls=%fused_computation.11.clone.1 | convolution fusion | flops 269484032 | bytes 1197060 | tf_op jit(solution)/shard_map/while/body/eval_jaxpr/dot_general | solution.py:21
  115.4 0.7 dynamic_slice.6
  116.7 2.0 %fusion.25 = f32[20,256,128]{2,1,0:T(8,128)S(1)} fusion(f32[20,256,128]{2,1,0:T(8,128)S(1)} %get-tuple-element.96, s32[]{:T(128)S(6)} %copy.20, bf16[4096,128]{1,0:T(8,128)(2,1)} %get-tuple-element.106, s32[4096]{0:T(1024)S(1)} %get-tuple-element.104, s32[256]{0:T(256)S(1)} %bitcast.48), kind=kOutput, calls=%fused_computation.11.clone.1 | convolution fusion | flops 269484032 | bytes 1197060 | tf_op jit(solution)/shard_map/while/body/eval_jaxpr/dot_general | solution.py:21
  118.8 0.7 dynamic_slice.6
  120.1 2.0 %fusion.25 = f32[20,256,128]{2,1,0:T(8,128)S(1)} fusion(f32[20,256,128]{2,1,0:T(8,128)S(1)} %get-tuple-element.96, s32[]{:T(128)S(6)} %copy.20, bf16[4096,128]{1,0:T(8,128)(2,1)} %get-tuple-element.106, s32[4096]{0:T(1024)S(1)} %get-tuple-element.104, s32[256]{0:T(256)S(1)} %bitcast.48), kind=kOutput, calls=%fused_computation.11.clone.1 | convolution fusion | flops 269484032 | bytes 1197060 | tf_op jit(solution)/shard_map/while/body/eval_jaxpr/dot_general | solution.py:21
  122.1 0.7 dynamic_slice.6
  123.5 2.0 %fusion.25 = f32[20,256,128]{2,1,0:T(8,128)S(1)} fusion(f32[20,256,128]{2,1,0:T(8,128)S(1)} %get-tuple-element.96, s32[]{:T(128)S(6)} %copy.20, bf16[4096,128]{1,0:T(8,128)(2,1)} %get-tuple-element.106, s32[4096]{0:T(1024)S(1)} %get-tuple-element.104, s32[256]{0:T(256)S(1)} %bitcast.48), kind=kOutput, calls=%fused_computation.11.clone.1 | convolution fusion | flops 269484032 | bytes 1197060 | tf_op jit(solution)/shard_map/while/body/eval_jaxpr/dot_general | solution.py:21
  125.5 0.7 dynamic_slice.6
  126.9 2.0 %fusion.25 = f32[20,256,128]{2,1,0:T(8,128)S(1)} fusion(f32[20,256,128]{2,1,0:T(8,128)S(1)} %get-tuple-element.96, s32[]{:T(128)S(6)} %copy.20, bf16[4096,128]{1,0:T(8,128)(2,1)} %get-tuple-element.106, s32[4096]{0:T(1024)S(1)} %get-tuple-element.104, s32[256]{0:T(256)S(1)} %bitcast.48), kind=kOutput, calls=%fused_computation.11.clone.1 | convolution fusion | flops 269484032 | bytes 1197060 | tf_op jit(solution)/shard_map/while/body/eval_jaxpr/dot_general | solution.py:21
  128.9 0.7 dynamic_slice.6
  130.3 2.0 %fusion.25 = f32[20,256,128]{2,1,0:T(8,128)S(1)} fusion(f32[20,256,128]{2,1,0:T(8,128)S(1)} %get-tuple-element.96, s32[]{:T(128)S(6)} %copy.20, bf16[4096,128]{1,0:T(8,128)(2,1)} %get-tuple-element.106, s32[4096]{0:T(1024)S(1)} %get-tuple-element.104, s32[256]{0:T(256)S(1)} %bitcast.48), kind=kOutput, calls=%fused_computation.11.clone.1 | convolution fusion | flops 269484032 | bytes 1197060 | tf_op jit(solution)/shard_map/while/body/eval_jaxpr/dot_general | solution.py:21
  132.3 1.3 multiply_reduce_fusion.1
  133.5 4.7 %gather_fusion = f32[20,256,128]{2,1,0:T(8,128)} fusion(f32[40,256,128]{2,1,0:T(8,128)} %bitcast.34, s32[1024]{0:T(1024)S(1)} %pad_clamp_fusion), kind=kCustom, calls=%fused_computation | custom fusion | bytes 5242960 | tf_op jit(solution)/shard_map/gather | solution.py:67
  138.2 33.6 %psum.7 = f32[]{:T(128)} all-reduce(f32[]{:T(128)} %multiply_reduce_fusion.1), channel_id=1, replica_groups=mesh['rep'=2,'shard'=16] {'shard'}, use_global_device_ids=true, to_apply=%region_5.6 | all-reduce | flops 1 | bytes 8 | tf_op jit(solution)/shard_map/psum | solution.py:69
  172.6 0.7 multiply_reduce_fusion
  173.4 0.7 scatter_custom_fusion.1
  174.0 0.6 copy.16
  174.7 3.3 %divide_subtract_fusion = f32[20,256,128]{2,1,0:T(8,128)} fusion(f32[20,256,128]{2,1,0:T(8,128)} %gather_fusion, f32[20,256,128]{2,1,0:T(8,128)S(1)} %get-tuple-element.34, f32[20,256]{1,0:T(8,128)S(1)} %fusion.17, f32[]{:T(128)S(6)} %div.33), kind=kLoop, calls=%fused_computation.13 | loop fusion | flops 3276800 | bytes 7884804 | tf_op jit(solution)/shard_map/sub | solution.py:29
  178.0 7.6 %scatter_fusion = f32[40,256,128]{2,1,0:T(8,128)} fusion(f32[40,256,128]{2,1,0:T(8,128)} %bitcast.35, s32[20]{0:T(128)S(1)} %fusion.18, f32[20,256,128]{2,1,0:T(8,128)} %divide_subtract_fusion), kind=kCustom, calls=%fused_computation.3 | custom fusion | bytes 7864400 | tf_op jit(solution)/shard_map/scatter | solution.py:72
  (37 shorter events, 0.2 us)
Async XLA Ops:
  7.2 36.7 %copy-start = (s32[640]{0:T(1024)S(1)}, s32[640]{0:T(1024)}, u32[]{:S(2)}) copy-start(s32[640]{0:T(1024)} %param.11) | copy-start | bytes 7684
  7.2 4.3 %copy-start.3 = (s32[1,1,16,128]{3,2,1,0:T(8,128)S(1)}, s32[1,1,16,128]{3,2,1,0:T(8,128)}, u32[]{:S(2)}) copy-start(s32[1,1,16,128]{3,2,1,0:T(8,128)} %param.8) | copy-start | bytes 24580
  7.2 21.6 %copy-start.4 = (s32[1,20]{1,0:T(1,128)S(1)}, s32[1,20]{1,0:T(1,128)}, u32[]{:S(2)}) copy-start(s32[1,20]{1,0:T(1,128)} %param.10) | copy-start | bytes 244
  7.2 21.6 %copy-start.2 = (f32[10240]{0:T(1024)S(1)}, f32[10240]{0:T(1024)}, u32[]{:S(2)}) copy-start(f32[10240]{0:T(1024)} %param.13) | copy-start | bytes 122884
  25.1 17.8 %all-to-all-start.1 = ((bf16[1,1,16,128,128]{4,3,1,0,2:T(8,128)(2,1)}), bf16[1,1,16,128,128]{4,3,1,0,2:T(8,128)(2,1)S(1)}, u32[]{:S(2)}, u32[]{:S(2)}) async-start(bf16[1,1,16,128,128]{4,3,1,0,2:T(8,128)(2,1)} %bitcast.9), calls=%async_computation.1 | async-start | bytes 1048576 | tf_op jit(solution)/shard_map/all_to_all | solution.py:53
  28.7 36.0 %all-gather.2.cloned.1.call-start = ((), (), s32[]{:S(2)}) async-start(), calls=%async_computation.2 | async-start | bytes 1572864 | tf_op jit(solution)/shard_map/all_gather | solution.py:57
  42.9 0.8 copy-start.1
Sparse Core Ops, SparseCore 0:
  43.9 20.7 all-gather.1
where the time goes:
time: 194 us; the launch traced here: 192 us
  blocking collectives  51.6 us (27%)
  local copies, waits for them, and re-layouts  48.6 us (25%)
  matrix products  39.7 us (20%)
  between operations  14.9 us (8%)
  loops' own time  14.4 us (7%)
  waiting for transfers between devices  12.9 us (7%)
  other arithmetic  6.55 us (3%)
  starting transfers between devices  3.62 us (2%)
    dot_general x20, matrix products, single_block(): return jnp.dot(onehot, gradients, preferred_element_type=jnp.float32)  39.7 us
    psum x1, blocking collectives, body(): square_sum = lax.psum(jnp.sum(blocks * blocks), 'shard')  33.6 us
    gather x1, local copies, waits for them, and re-layouts, slot_blocks(): local_block = block_home[safe_ids // BLOCK] % blocks_here  16.7 us
    another operation x1, loops' own time, block_sums(): return lax.map(single_block, jnp.arange(touch_count, dtype=jnp.int32))  14.4 us
    all_to_all x1, blocking collectives, body(): lax.all_to_all(row_ids, 'shard', split_axis=2, concat_axis=2, tiled=True)  13.6 us
    dynamic_slice x20, local copies, waits for them, and re-layouts, block_sums(): return lax.map(single_block, jnp.arange(touch_count, dtype=jnp.int32))  13.3 us
    all_to_all x1, waiting for transfers between devices, body(): lax.all_to_all(grad_rows, 'shard', split_axis=2, concat_axis=2, tiled=True)  9.16 us
    scatter x1, local copies, waits for them, and re-layouts, body(): table_out = table_blocks.at[listed].set(new_rows).reshape(-1, feature_width)  7.6 us
  transfers between devices with their start and end apart: 2, of which 2 were waited for; matrix products, arithmetic and copies ran while one was open for 9% of the time, Pallas kernels for 0%

commit v1 on v0

v1 whole, which is shorter than its diff:
```python
import functools
import math

import jax
import jax.numpy as jnp
from jax import lax
from jax.experimental import pallas as pl
from jax.experimental.pallas import tpu as pltpu
from jax.sharding import PartitionSpec as P

BLOCK = 256
CLIP_RMS = 0.25
LEARN_RATE = 0.1
DECAY_RATE = 0.05
LANES = 128
META = 8
PARTS = BLOCK // LANES
TILE = 2 * LANES
MIB = 1 << 20
WHOLE = 67043328


VMEM = pl.BlockSpec(memory_space=pltpu.VMEM)
HBM = pl.BlockSpec(memory_space=pltpu.HBM)


def call(kernel, us, mib, **kwargs):
    return pl.pallas_call(
        kernel,
        compiler_params=pltpu.CompilerParams(vmem_limit_bytes=int(min(mib * MIB, WHOLE))),
        cost_estimate=pl.CostEstimate(
            flops=int(us * 4e6), bytes_accessed=MIB, transcendentals=0
        ),
        **kwargs,
    )


def like(shape, dtype=jnp.float32):
    return jax.ShapeDtypeStruct(shape, dtype)


def pack_kernel(slots, ids_hbm, grads_hbm, out_ref, ids_ref, sems):
    groups = ids_ref.shape[0]
    fetch = pltpu.make_async_copy(ids_hbm, ids_ref, sems.at[0])
    copy = pltpu.make_async_copy(grads_hbm, out_ref.at[:, pl.ds(0, slots), :], sems.at[1])
    fetch.start()
    copy.start()
    row = lax.broadcasted_iota(jnp.int32, (META, LANES), 0)
    fetch.wait()
    for group in range(groups):
        ids = jnp.broadcast_to(ids_ref[group : group + 1, :], (META, LANES))
        top = jnp.where(ids >= 0, ids >> 16, -1)
        digits = jnp.where(
            row == 0, top, jnp.where(row == 1, (ids >> 8) & 255, ids & 255)
        )
        out_ref[group, slots : slots + META, :] = digits.astype(jnp.float32).astype(
            jnp.bfloat16
        )
    copy.wait()


def pack(ids, grads):
    groups, slots, width = grads.shape
    pad = LANES - slots
    ids = jnp.pad(ids, ((0, 0), (0, pad)), constant_values=-1) if pad else ids
    return call(
        functools.partial(pack_kernel, slots),
        1.0,
        64,
        out_shape=like((groups, slots + META, width), grads.dtype),
        in_specs=[HBM, HBM],
        out_specs=VMEM,
        scratch_shapes=[
            pltpu.VMEM((groups, LANES), jnp.int32),
            pltpu.SemaphoreType.DMA((2,)),
        ],
    )(ids, grads)


def keep_kernel(touched_hbm, table_hbm, out_hbm, listed, bounce, other, sems):
    blocks, touch = table_hbm.shape[0], touched_hbm.shape[1]
    fetch = pltpu.make_async_copy(touched_hbm, listed, sems.at[0])
    fetch.start()

    def clear(b, _):
        other[b] = 0
        return 0

    lax.fori_loop(0, blocks, clear, 0)
    fetch.wait()

    def mark(t, _):
        other[listed[0, t]] = 1
        return 0

    lax.fori_loop(0, touch, mark, 0)

    def pull(b, count):
        free = other[b] == 0

        @pl.when(free)
        def _():
            pltpu.make_async_copy(table_hbm.at[b], bounce.at[count], sems.at[1]).start()
            other[blocks + count] = b

        return count + free.astype(jnp.int32)

    lax.fori_loop(0, blocks, pull, 0)
    pltpu.make_async_copy(bounce, bounce, sems.at[1]).wait()

    def put(j, _):
        b = other[blocks + j]
        pltpu.make_async_copy(bounce.at[j], out_hbm.at[b], sems.at[2]).start()
        return 0

    lax.fori_loop(0, blocks - touch, put, 0)
    pltpu.make_async_copy(bounce, bounce, sems.at[2]).wait()


def keep_untouched(touched, table):
    blocks, _, width = table.shape
    touch = touched.shape[1]
    return call(
        keep_kernel,
        4.0,
        64,
        out_shape=like(table.shape, table.dtype),
        in_specs=[HBM, HBM],
        out_specs=HBM,
        scratch_shapes=[
            pltpu.SMEM((1, touch), jnp.int32),
            pltpu.VMEM((blocks - touch, BLOCK, width), table.dtype),
            pltpu.SMEM((2 * blocks,), jnp.int32),
            pltpu.SemaphoreType.DMA((3,)),
        ],
    )(touched, table)


def keys_kernel(slots, blocks_here, touched_hbm, home_hbm, data_ref, keys_ref, listed, home_ref, sems):
    a = pltpu.make_async_copy(touched_hbm, listed, sems.at[0])
    b = pltpu.make_async_copy(home_hbm, home_ref, sems.at[1])
    a.start()
    b.start()
    groups, touch = data_ref.shape[0], listed.shape[1]
    per = LANES // slots
    lane = lax.broadcasted_iota(jnp.int32, (1, LANES), 1)
    meta = data_ref[:, slots : slots + META, :].astype(jnp.float32)
    top, mid, low = (meta[:, i, :].astype(jnp.int32) for i in range(3))
    block = top * 256 + mid
    lo, hi = block & (LANES - 1), block >> 7
    home = jnp.zeros_like(block)
    a.wait()
    b.wait()
    for r in range(home_ref.shape[0]):
        line = jnp.broadcast_to(home_ref[r : r + 1, :], block.shape)
        found = jnp.take_along_axis(line, lo, axis=1)
        home = jnp.where(hi == r, found, home)
    local = jnp.where(top >= 0, home - lax.axis_index("shard") * blocks_here, -1)
    keys = jnp.full_like(block, -1)
    for t in range(touch):
        keys = jnp.where(local == listed[0, t], t * BLOCK + low, keys)
    if per == 1:
        keys_ref[...] = keys
        return
    for g in range(groups // per):
        line = keys[g * per : g * per + 1, :]
        for j in range(1, per):
            key = pltpu.roll(keys[g * per + j : g * per + j + 1, :], j * slots, 1)
            line = jnp.where((lane >= j * slots) & (lane < (j + 1) * slots), key, line)
        keys_ref[g : g + 1, :] = line


def slot_keys(touched, home, data, slots, blocks_here):
    groups = data.shape[0]
    return call(
        functools.partial(keys_kernel, slots, blocks_here),
        1.0,
        4,
        out_shape=like((groups * slots // LANES, LANES), jnp.int32),
        in_specs=[HBM, HBM, VMEM],
        out_specs=VMEM,
        scratch_shapes=[
            pltpu.SMEM(touched.shape, jnp.int32),
            pltpu.VMEM(home.shape, jnp.int32),
            pltpu.SemaphoreType.DMA((2,)),
        ],
    )(touched, home, data)


def add_rows(slots, fresh, squared, first, keys_ref, data_ref, *refs):
    sums_ref, weights = refs[0 if fresh else 1], refs[-1]
    touch, _, width = sums_ref.shape
    per = TILE // slots
    tiles = data_ref.shape[0] // per
    many = next(m for m in (4, 2, 1) if touch % m == 0)
    key_rows = []
    for k in range(tiles):
        at = first + 2 * k
        pair = [keys_ref[at + i : at + i + 1, :] for i in range(2)]
        upper = [((key >> 7) & 1).astype(jnp.float32) for key in pair]
        upper = [jnp.broadcast_to(u, (LANES, LANES)).T for u in upper]
        upper = jnp.concatenate(upper, axis=0).astype(jnp.bfloat16)
        rows = data_ref[k * per : (k + 1) * per, 0:slots, :].reshape(TILE, width)
        high = rows * upper
        weights[k, :, width : 2 * width] = high
        weights[k, :, 0:width] = rows - high
        flat = [jnp.where(key >= 0, (key >> 8) * LANES + (key & (LANES - 1)), -1) for key in pair]
        key_rows.append(jnp.concatenate(flat, axis=1))
    row = lax.broadcasted_iota(jnp.int32, (many * LANES, TILE), 0)

    def step(u, carry):
        total = None
        for k in range(tiles):
            match = row == jnp.broadcast_to(key_rows[k] - u * (many * LANES), row.shape)
            onehot = jnp.where(match, 1.0, 0.0).astype(jnp.bfloat16)
            part = jnp.dot(onehot, weights[k], preferred_element_type=jnp.float32)
            total = part if total is None else total + part
        for i in range(many):
            t = u * many + i
            for p in range(PARTS):
                piece = total[i * LANES : (i + 1) * LANES, p * width : (p + 1) * width]
                at = pl.ds(p * LANES, LANES)
                piece = piece if fresh else piece + sums_ref[t, at, :]
                sums_ref[t, at, :] = piece
                if squared:
                    carry = carry + jnp.sum((piece * piece).reshape(-1, 8, width), axis=0)
        return carry

    carry = jnp.zeros((8, width), jnp.float32) if squared else 0
    carry = lax.fori_loop(0, touch // many, step, carry)
    if squared:
        refs[-2][...] = carry


def sums_of(keys, data, slots, touch, first=0, sums=None, squared=False):
    width = data.shape[-1]
    fresh = sums is None
    return call(
        functools.partial(add_rows, slots, fresh, squared, first),
        data.shape[0] * slots / 512,
        10,
        out_shape=(like((touch, BLOCK, width)), like((8, width)))[: 1 + squared],
        in_specs=[VMEM] * (2 if fresh else 3),
        out_specs=(VMEM, VMEM)[: 1 + squared],
        scratch_shapes=[
            pltpu.VMEM((data.shape[0] * slots // TILE, TILE, 2 * width), data.dtype)
        ],
        input_output_aliases={} if fresh else {2: 0},
    )(keys, data, *([] if fresh else [sums]))


def spread_kernel(touched_hbm, accum_hbm, rep_ref, listed, accum, sems):
    a = pltpu.make_async_copy(touched_hbm, listed, sems.at[0])
    b = pltpu.make_async_copy(accum_hbm, accum, sems.at[1])
    a.start()
    b.start()
    a.wait()
    b.wait()

    def step(t, _):
        for part in range(PARTS):
            row = accum[pl.ds(listed[0, t] * PARTS + part, 1), :]
            rep_ref[t, part * LANES : (part + 1) * LANES, :] = jnp.broadcast_to(
                row, (LANES, LANES)
            ).T
        return 0

    lax.fori_loop(0, rep_ref.shape[0], step, 0)


def spread_accum(touched, accum):
    touch = touched.shape[1]
    return call(
        spread_kernel,
        2.0,
        8,
        out_shape=like((touch, BLOCK, LANES)),
        in_specs=[HBM, HBM],
        out_specs=VMEM,
        scratch_shapes=[
            pltpu.SMEM((1, touch), jnp.int32),
            pltpu.VMEM(accum.shape, accum.dtype),
            pltpu.SemaphoreType.DMA((2,)),
        ],
    )(touched, accum)


def means_kernel(touched_hbm, sums_ref, rep_ref, flat_ref, listed, turned, sem):
    touch, _, width = sums_ref.shape
    fetch = pltpu.make_async_copy(touched_hbm, listed, sem)
    fetch.start()
    flat_ref[...] = jnp.zeros_like(flat_ref)
    lane = lax.broadcasted_iota(jnp.int32, (LANES, LANES), 1)

    def step(t, gathered):
        total = sums_ref[t]
        square = total * total * (1.0 / width)
        wide = jnp.broadcast_to(jnp.sum(square, axis=1, keepdims=True), (BLOCK, LANES))
        rep_ref[t] = wide
        for part in range(PARTS):
            piece = wide[part * LANES : (part + 1) * LANES, :]
            gathered = jnp.where(lane == t * PARTS + part, piece, gathered)
        return gathered

    gathered = lax.fori_loop(0, touch, step, jnp.zeros((LANES, LANES), jnp.float32))
    turned[...] = gathered.T
    fetch.wait()
    for t in range(touch):
        for part in range(PARTS):
            j = t * PARTS + part
            flat_ref[pl.ds(listed[0, t] * PARTS + part, 1), :] = turned[j : j + 1, :]


def row_means(touched, sums, accum_rows):
    touch = touched.shape[1]
    assert touch * PARTS <= LANES
    return call(
        means_kernel,
        2.0,
        8,
        out_shape=(like((touch, BLOCK, LANES)), like((accum_rows, LANES))),
        in_specs=[HBM, VMEM],
        out_specs=(VMEM, VMEM),
        scratch_shapes=[
            pltpu.SMEM((1, touch), jnp.int32),
            pltpu.VMEM((LANES, LANES), jnp.float32),
            pltpu.SemaphoreType.DMA,
        ],
    )(touched, sums)


def add_kernel(*refs):
    total = refs[0][...]
    for ref in refs[1:-1]:
        total = total + ref[...]
    refs[-1][...] = total


def add_all(parts):
    return call(
        add_kernel,
        0.2,
        1,
        out_shape=like(parts[0].shape),
        in_specs=[VMEM] * len(parts),
        out_specs=VMEM,
    )(*parts)


def update_kernel(limit, touched_hbm, *refs):
    out_hbm, new_accum_ref, fresh, listed, sems = refs[-5:]
    sums_ref, table_ref, accum_rep_ref, mean_rep_ref, accum_ref, mean_ref = refs[-12:-6]
    fetch = pltpu.make_async_copy(touched_hbm, listed, sems.at[0])
    fetch.start()
    square = refs[0][...]
    for ref in refs[1:-12]:
        square = square + ref[...]
    square = jnp.sum(jnp.sum(square, axis=1, keepdims=True), axis=0, keepdims=True)
    factor = limit / jnp.maximum(jnp.sqrt(square), limit)
    factor_sq = factor * factor
    new_accum_ref[...] = accum_ref[...] + factor_sq * mean_ref[...]
    rate = LEARN_RATE * factor
    fetch.wait()

    def step(t, _):
        accum = accum_rep_ref[t] + factor_sq * mean_rep_ref[t]
        old = table_ref[listed[0, t]]
        fresh[t] = old * (1.0 - DECAY_RATE) - (rate * sums_ref[t]) * lax.rsqrt(accum)
        pltpu.make_async_copy(fresh.at[t], out_hbm.at[listed[0, t]], sems.at[1]).start()
        return 0

    lax.fori_loop(0, fresh.shape[0], step, 0)
    pltpu.make_async_copy(fresh, fresh, sems.at[1]).wait()


def update(limit, touched, squares, sums, old, accum_rep, mean_rep, accum, mean, table):
    n = len(squares)
    return call(
        functools.partial(update_kernel, limit),
        2.5,
        8,
        out_shape=(like(table.shape, table.dtype), like(accum.shape, accum.dtype)),
        in_specs=[HBM] + [VMEM] * (n + 6) + [HBM],
        out_specs=(HBM, VMEM),
        scratch_shapes=[
            pltpu.VMEM(sums.shape, table.dtype),
            pltpu.SMEM(touched.shape, jnp.int32),
            pltpu.SemaphoreType.DMA((2,)),
        ],
        input_output_aliases={n + 7: 0},
    )(touched, *squares, sums, old, accum_rep, mean_rep, accum, mean, table)


def step(row_ids, grad_rows, touched, block_home, embed_table, row_accum):
    slots, width = grad_rows.shape[3:]
    blocks_here = embed_table.shape[0] // BLOCK
    touch = touched.shape[1]
    shards = lax.axis_size("shard")
    reps = lax.axis_size("rep")
    limit = CLIP_RMS * math.sqrt(shards * touch * BLOCK * width)
    swap = [(i, (i + 1) % reps) for i in range(reps)]
    ids, grads = row_ids[0, 0], grad_rows[0, 0]
    table = embed_table.reshape(blocks_here, BLOCK, width)
    accum = row_accum.reshape(-1, LANES)
    home = jnp.pad(block_home, (0, -block_home.shape[0] % LANES)).reshape(-1, LANES)

    data = pack(ids, grads)
    data = lax.all_to_all(data, "shard", 0, 0, tiled=True)
    table_out = keep_untouched(touched, table)
    split = shards // 2
    other_a = lax.ppermute(data[:split], "rep", swap)
    other_b = lax.ppermute(data[split:], "rep", swap)
    keys = slot_keys(touched, home, data, slots, blocks_here)
    other_keys = lax.ppermute(keys, "rep", swap)
    (sums,) = sums_of(keys, data, slots, touch)
    accum_rep = spread_accum(touched, accum)
    (sums,) = sums_of(other_keys, other_a, slots, touch, 0, sums)
    first = split * slots // LANES
    sums, square = sums_of(other_keys, other_b, slots, touch, first, sums, True)
    squares = [square]
    stride = 1
    while stride < shards:
        fan = min(4, shards // stride)
        if len(squares) > 1:
            squares = [add_all(squares)]
        squares += [
            lax.ppermute(
                squares[0], "shard", [(i, i ^ (r * stride)) for i in range(shards)]
            )
            for r in range(1, fan)
        ]
        stride *= fan
    mean_rep, mean = row_means(touched, sums, accum.shape[0])
    table_out, accum_out = update(
        limit, touched, squares, sums, table, accum_rep, mean_rep, accum, mean, table_out
    )
    return table_out.reshape(-1, width), accum_out.reshape(-1)


def solution(mesh):
    shards = mesh.shape["shard"]
    assert mesh.shape["rep"] == 2 and shards & (shards - 1) == 0
    in_specs = (
        P("rep", "shard", None, None),
        P("rep", "shard", None, None, None),
        P("shard", None),
        P(),
        P("shard", None),
        P("shard"),
    )
    out_specs = (P("shard", None), P("shard"))
    return jax.shard_map(
        step, mesh=mesh, in_specs=in_specs, out_specs=out_specs, check_vma=False
    )
```

time: 194 us -> 76.6 us (0.39)
  matrix products: 39.7 us -> 0 us
  local copies, waits for them, and re-layouts: 48.6 us -> 10.1 us
  blocking collectives: 51.6 us -> 24.1 us
  Pallas kernels: 0 us -> 24.2 us
  loops' own time: 14.4 us -> 0 us
  between operations: 14.9 us -> 0.8 us
  other arithmetic: 6.55 us -> 0 us
  starting transfers between devices: 3.62 us -> 9.92 us
  waiting for transfers between devices: 12.9 us -> 7.1 us
    dot_general x20 -> x0, matrix products: 39.7 us -> none  [single_block(): return jnp.dot(onehot, gradients, preferred_element_type=jnp.float32)]
    psum x1 -> x0, blocking collectives: 33.6 us -> none  [body(): square_sum = lax.psum(jnp.sum(blocks * blocks), 'shard')]
    pallas_call x0 -> x10, Pallas kernels: none -> 24.2 us  [the longest x3 8.5 us: sums_of(): call(functools.partial(add_rows, slots, fresh, squared, first), data.shap...]
    gather x3 -> x0, local copies, waits for them, and re-layouts: 22 us -> none  [the longest x1 16.7 us: slot_blocks(): local_block = block_home[safe_ids // BLOCK] % blocks_here]
    another operation x1 -> x0, loops' own time: 14.4 us -> none  [block_sums(): return lax.map(single_block, jnp.arange(touch_count, dtype=jnp.int32))]
    dynamic_slice x20 -> x0, local copies, waits for them, and re-layouts: 13.3 us -> none  [block_sums(): return lax.map(single_block, jnp.arange(touch_count, dtype=jnp.int32))]
    all_to_all x1, blocking collectives: 13.6 us -> 24.1 us  [step(): data = lax.all_to_all(data, 'shard', 0, 0, tiled=True)]
    ppermute x0 -> x9, starting transfers between devices: none -> 9.92 us  [the longest x6 6.25 us: step(): lax.ppermute(squares[0], 'shard', [(i, i ^ r * stride) for i in range(sha...]
  transfers between devices with their start and end apart: 2 -> 9, of which waited for: 2 -> 3; matrix products, arithmetic and copies ran while one was open for 9% -> 0% of each run, Pallas kernels for 0% -> 21%
where the time goes in v1:
time: 76.6 us; the launch traced here: 76.1 us
  Pallas kernels  24.2 us (32%)
  blocking collectives  24.1 us (31%)
  local copies, waits for them, and re-layouts  10.1 us (13%)
  starting transfers between devices  9.92 us (13%)
  waiting for transfers between devices  7.1 us (9%)
  between operations  0.8 us (1%)
    all_to_all x1, blocking collectives, step(): data = lax.all_to_all(data, 'shard', 0, 0, tiled=True)  24.1 us
    unnamed x22, local copies, waits for them, and re-layouts  10 us
    pallas_call x3, Pallas kernels, sums_of(): call(functools.partial(add_rows, slots, fresh, squared, first), data.shap...  8.5 us
    ppermute x6, starting transfers between devices, step(): lax.ppermute(squares[0], 'shard', [(i, i ^ r * stride) for i in range(sha...  6.25 us
    ppermute x1, waiting for transfers between devices, step(): other_keys = lax.ppermute(keys, 'rep', swap)  5.33 us
    pallas_call x1, Pallas kernels, keep_untouched(): call(keep_kernel, 4.0, 64, out_shape=like(table.shape, table.dtype), in_s...  4.12 us
    pallas_call x1, Pallas kernels, update(): call(functools.partial(update_kernel, limit), 2.5, 8, out_shape=(like(tab...  3.41 us
    pallas_call x1, Pallas kernels, spread_accum(): call(spread_kernel, 2.0, 8, out_shape=like((touch, BLOCK, LANES)), in_spe...  2.57 us
  transfers between devices with their start and end apart: 9, of which 3 were waited for; matrix products, arithmetic and copies ran while one was open for 0% of the time, Pallas kernels for 21%

profile of v1, /device:TPU:0, one launch (start us, length us, event | category | flops | bytes accessed | tf_op | source)
XLA Modules:
  0.0 76.1 jit_solution(6795223930607775161)
XLA Ops:
  0.6 1.9 %shard_map.77 = bf16[16,136,128]{2,1,0:T(8,128)(2,1)} custom-call(s32[16,128]{1,0:T(8,128)} %bitcast.14, bf16[16,128,128]{2,1,0:T(8,128)(2,1)} %bitcast.13), custom_call_target="tpu_custom_call" | custom-call | flops 4000000 | bytes 1048576 | tf_op jit(solution)/shard_map/pallas_call | solution.py:66
  2.5 24.1 %all_to_all.5.data_ref = bf16[16,136,128]{2,1,0:T(8,128)(2,1)S(1)} all-to-all(bf16[16,136,128]{2,1,0:T(8,128)(2,1)} %shard_map.77), channel_id=1, replica_groups=mesh['rep'=2,'shard'=16] {'shard'}, dimensions={0} | all-to-all | bytes 1114112 | tf_op jit(solution)/shard_map/all_to_all | solution.py:408
  26.6 1.6 %collective-permute-start.2 = (bf16[8,136,128]{2,1,0:T(8,128)(2,1)S(1)}, bf16[8,136,128]{2,1,0:T(8,128)(2,1)S(1)}, u32[]{:S(2)}, u32[]{:S(2)}) collective-permute-start(bf16[8,136,128]{2,1,0:T(8,128)(2,1)S(1)} %get-tuple-element.14), channel_id=1, source_target_pairs={{0,16},{16,0},{1,17},{17,1},{2,18},{18,2},{3,19},{19,3},{4,20},{20... | collective-permute-start | bytes 835592 | tf_op jit(solution)/shard_map/ppermute | solution.py:411
  28.2 0.5 collective-permute-start.1
  28.7 0.0 copy-start.7
  28.7 0.7 copy-done.7
  29.4 0.0 copy-start.10
  29.4 0.7 copy-done.10
  30.1 0.8 shard_map.78.keys_ref
  30.8 1.6 %collective-permute-start = (s32[16,128]{1,0:T(8,128)S(1)}, s32[16,128]{1,0:T(8,128)S(1)}, u32[]{:S(2)}, u32[]{:S(2)}) collective-permute-start(s32[16,128]{1,0:T(8,128)S(1)} %shard_map.78.keys_ref), channel_id=1, source_target_pairs={{0,16},{16,0},{1,17},{17,1},{2,18},{18,2},{3,19},{19,3},{4,20},{20... | collective-permute-start | bytes 24584 | tf_op jit(solution)/shard_map/ppermute | solution.py:414
  32.4 3.8 %shard_map.79.refs_0_ = f32[20,256,128]{2,1,0:T(8,128)S(1)} custom-call(s32[16,128]{1,0:T(8,128)S(1)} %shard_map.78.keys_ref, bf16[16,136,128]{2,1,0:T(8,128)(2,1)S(1)} %all_to_all.5.data_ref), custom_call_target="tpu_custom_call" | custom-call | flops 16000000 | bytes 1048576 | tf_op jit(solution)/shard_map/pallas_call | solution.py:238
  36.2 5.3 %collective-permute-done.keys_ref = s32[16,128]{1,0:T(8,128)S(1)} collective-permute-done((s32[16,128]{1,0:T(8,128)S(1)}, s32[16,128]{1,0:T(8,128)S(1)}, u32[]{:S(2)}, u32[]{:S(2)}) %collective-permute-start) | collective-permute-done | bytes 8224 | tf_op jit(solution)/shard_map/ppermute | solution.py:414
  41.5 0.0 collective-permute-done.2.data_ref
  41.5 2.4 %shard_map.80.refs_0_ = f32[20,256,128]{2,1,0:T(8,128)S(1)} custom-call(s32[16,128]{1,0:T(8,128)S(1)} %collective-permute-done.keys_ref, bf16[8,136,128]{2,1,0:T(8,128)(2,1)S(1)} %collective-permute-done.2.data_ref, f32[20,256,128]{2,1,0:T(8,128)S(1)} %shard_map.79.refs_0_), custom_call_target="tpu_custom_call", output_to_operand_aliasing={{}: (2, {})} | custom-call | flops 8000000 | bytes 1048576 | tf_op jit(solution)/shard_map/pallas_call | solution.py:238
  43.9 0.0 copy-start.5
  43.9 0.0 copy-start.8
  43.9 0.0 collective-permute-done.1.data_ref
  43.9 2.4 %shard_map.81 = (f32[20,256,128]{2,1,0:T(8,128)S(1)}, f32[8,128]{1,0:T(8,128)S(1)}) custom-call(s32[16,128]{1,0:T(8,128)S(1)} %collective-permute-done.keys_ref, bf16[8,136,128]{2,1,0:T(8,128)(2,1)S(1)} %collective-permute-done.1.data_ref, f32[20,256,128]{2,1,0:T(8,128)S(1)} %shard_map.80.refs_0_), custom_call_target="tpu_custom_call", output_to_operand_aliasing={{0}: (2, {})} | custom-call | flops 8000000 | bytes 1048576 | tf_op jit(solution)/shard_map/pallas_call | solution.py:238
  46.3 0.0 copy-start
  46.3 1.5 %copy-done = f32[20,256,128]{2,1,0:T(8,128)} copy-done((f32[20,256,128]{2,1,0:T(8,128)}, f32[20,256,128]{2,1,0:T(8,128)S(1)}, u32[]{:S(2)}) %copy-start) | copy-done | bytes 2621464
  47.8 0.0 collective-permute-start.5
  47.8 0.9 %collective-permute-start.4 = (f32[8,128]{1,0:T(8,128)S(1)}, f32[8,128]{1,0:T(8,128)S(1)}, u32[]{:S(2)}, u32[]{:S(2)}) collective-permute-start(f32[8,128]{1,0:T(8,128)S(1)} %get-tuple-element.8.refs_0_), channel_id=1, source_target_pairs={{0,2},{1,3},{2,0},{3,1},{4,6},{5,7},{6,4},{7,5},{8,10},{9,11},{10,... | collective-permute-start | bytes 12296 | tf_op jit(solution)/shard_map/ppermute | solution.py:427
  48.7 1.0 %collective-permute-start.3 = (f32[8,128]{1,0:T(8,128)S(1)}, f32[8,128]{1,0:T(8,128)S(1)}, u32[]{:S(2)}, u32[]{:S(2)}) collective-permute-start(f32[8,128]{1,0:T(8,128)S(1)} %get-tuple-element.8.refs_0_), channel_id=1, source_target_pairs={{0,1},{1,0},{2,3},{3,2},{4,5},{5,4},{6,7},{7,6},{8,9},{9,8},{10,11... | collective-permute-start | bytes 12296 | tf_op jit(solution)/shard_map/ppermute | solution.py:427
  49.7 1.2 %collective-permute-done.5.refs_3_ = f32[8,128]{1,0:T(8,128)S(1)} collective-permute-done((f32[8,128]{1,0:T(8,128)S(1)}, f32[8,128]{1,0:T(8,128)S(1)}, u32[]{:S(2)}, u32[]{:S(2)}) %collective-permute-start.5) | collective-permute-done | bytes 4128 | tf_op jit(solution)/shard_map/ppermute | solution.py:427
  50.8 0.6 collective-permute-done.4.refs_2_
  51.4 0.0 collective-permute-done.3.refs_1_
  51.4 0.6 shard_map.82.refs_0_
  52.0 1.5 %collective-permute-start.8 = (f32[8,128]{1,0:T(8,128)}, f32[8,128]{1,0:T(8,128)}, u32[]{:S(2)}, u32[]{:S(2)}) collective-permute-start(f32[8,128]{1,0:T(8,128)} %shard_map.82.refs_0_), channel_id=1, source_target_pairs={{0,12},{1,13},{2,14},{3,15},{4,8},{5,9},{6,10},{7,11},{8,4},{9,5},... | collective-permute-start | bytes 12296 | tf_op jit(solution)/shard_map/ppermute | solution.py:427
  53.5 0.6 collective-permute-start.7
  54.1 2.3 %collective-permute-start.6 = (f32[8,128]{1,0:T(8,128)}, f32[8,128]{1,0:T(8,128)}, u32[]{:S(2)}, u32[]{:S(2)}) collective-permute-start(f32[8,128]{1,0:T(8,128)} %shard_map.82.refs_0_), channel_id=1, source_target_pairs={{0,4},{1,5},{2,6},{3,7},{4,0},{5,1},{6,2},{7,3},{8,12},{9,13},{10,... | collective-permute-start | bytes 12296 | tf_op jit(solution)/shard_map/ppermute | solution.py:427
  56.4 0.0 copy-done.5
  56.4 0.0 copy-done.8
  56.4 2.6 %shard_map.83.refs_6_ = f32[20,256,128]{2,1,0:T(8,128)S(1)} custom-call(s32[1,20]{1,0:T(1,128)S(1)} %copy-done.8, f32[80,128]{1,0:T(8,128)S(1)} %bitcast.9), custom_call_target="tpu_custom_call" | custom-call | flops 8000000 | bytes 1048576 | tf_op jit(solution)/shard_map/pallas_call | solution.py:273
  59.0 0.0 copy-start.3
  59.0 1.5 %copy-done.3 = f32[20,256,128]{2,1,0:T(8,128)} copy-done((f32[20,256,128]{2,1,0:T(8,128)}, f32[20,256,128]{2,1,0:T(8,128)S(1)}, u32[]{:S(2)}) %copy-start.3) | copy-done | bytes 2621464
  60.5 4.1 %shard_map.85.refs_10_ = f32[40,256,128]{2,1,0:T(8,128)} custom-call(s32[1,20]{1,0:T(1,128)} %touched_hbm.9, f32[40,256,128]{2,1,0:T(8,128)} %bitcast.7), custom_call_target="tpu_custom_call" | custom-call | flops 16000000 | bytes 1048576 | tf_op jit(solution)/shard_map/pallas_call | solution.py:123
  64.7 0.0 copy-start.1
  64.7 1.7 %copy-done.1 = f32[20,256,128]{2,1,0:T(8,128)S(1)} copy-done((f32[20,256,128]{2,1,0:T(8,128)S(1)}, f32[20,256,128]{2,1,0:T(8,128)}, u32[]{:S(2)}) %copy-start.1) | copy-done | bytes 2621464
  66.4 0.0 copy-start.9
  66.4 0.7 copy-done.9
  67.1 0.0 copy-start.4
  67.1 2.3 %shard_map.84 = (f32[20,256,128]{2,1,0:T(8,128)S(1)}, f32[80,128]{1,0:T(8,128)S(1)}) custom-call(s32[1,20]{1,0:T(1,128)S(1)} %copy-done.9, f32[20,256,128]{2,1,0:T(8,128)S(1)} %copy-done.1), custom_call_target="tpu_custom_call" | custom-call | flops 8000000 | bytes 1048576 | tf_op jit(solution)/shard_map/pallas_call | solution.py:317
  69.4 0.0 collective-permute-done.8.refs_3_
  69.4 0.0 collective-permute-done.7.refs_2_
  69.4 0.0 collective-permute-done.6.refs_1_
  69.4 0.0 copy-done.4
  69.4 0.0 copy-start.2
  69.4 2.5 %copy-done.2 = f32[10240,128]{1,0:T(8,128)S(1)} copy-done((f32[10240,128]{1,0:T(8,128)S(1)}, f32[10240,128]{1,0:T(8,128)}, u32[]{:S(2)}) %copy-start.2) | copy-done | bytes 5242904
  71.9 0.0 copy-start.6
  71.9 0.8 %copy-done.6 = f32[10240]{0:T(1024)S(1)} copy-done((f32[10240]{0:T(1024)S(1)}, f32[10240]{0:T(1024)}, u32[]{:S(2)}) %copy-start.6) | copy-done | bytes 40984
  72.7 3.4 %shard_map.86 = (f32[40,256,128]{2,1,0:T(8,128)}, f32[80,128]{1,0:T(8,128)}) custom-call(s32[1,20]{1,0:T(1,128)S(1)} %copy-done.9, f32[8,128]{1,0:T(8,128)} %shard_map.82.refs_0_, f32[8,128]{1,0:T(8,128)} %collective-permute-done.6.refs_1_, f32[8,128]{1,0:T(8,128)} %collective-permute-done.7.refs_2_, ...), custom_call_target="tpu_custom_call", output_to_operand_aliasing={{0}: (11, {})} | custom-call | flops 10000000 | bytes 1048576 | tf_op jit(solution)/shard_map/pallas_call | solution.py:378
  (1 shorter events, 0.0 us)
Async XLA Ops:
  26.6 14.9 %collective-permute-start.2 = (bf16[8,136,128]{2,1,0:T(8,128)(2,1)S(1)}, bf16[8,136,128]{2,1,0:T(8,128)(2,1)S(1)}, u32[]{:S(2)}, u32[]{:S(2)}) collective-permute-start(bf16[8,136,128]{2,1,0:T(8,128)(2,1)S(1)} %get-tuple-element.14), channel_id=1, source_target_pairs={{0,16},{16,0},{1,17},{17,1},{2,18},{18,2},{3,19},{19,3},{4,20},{20... | collective-permute-start | bytes 835592 | tf_op jit(solution)/shard_map/ppermute | solution.py:411
  28.2 15.7 %collective-permute-start.1 = (bf16[8,136,128]{2,1,0:T(8,128)(2,1)S(1)}, bf16[8,136,128]{2,1,0:T(8,128)(2,1)S(1)}, u32[]{:S(2)}, u32[]{:S(2)}) collective-permute-start(bf16[8,136,128]{2,1,0:T(8,128)(2,1)S(1)} %get-tuple-element.15), channel_id=1, source_target_pairs={{0,16},{16,0},{1,17},{17,1},{2,18},{18,2},{3,19},{19,3},{4,20},{20... | collective-permute-start | bytes 835592 | tf_op jit(solution)/shard_map/ppermute | solution.py:412
  28.7 0.7 copy-start.7
  29.4 0.7 copy-start.10
  30.8 10.7 %collective-permute-start = (s32[16,128]{1,0:T(8,128)S(1)}, s32[16,128]{1,0:T(8,128)S(1)}, u32[]{:S(2)}, u32[]{:S(2)}) collective-permute-start(s32[16,128]{1,0:T(8,128)S(1)} %shard_map.78.keys_ref), channel_id=1, source_target_pairs={{0,16},{16,0},{1,17},{17,1},{2,18},{18,2},{3,19},{19,3},{4,20},{20... | collective-permute-start | bytes 24584 | tf_op jit(solution)/shard_map/ppermute | solution.py:414
  43.9 12.5 %copy-start.5 = (f32[10240]{0:T(1024)S(1)}, f32[10240]{0:T(1024)}, u32[]{:S(2)}) copy-start(f32[10240]{0:T(1024)} %param.11) | copy-start | bytes 122884
  43.9 12.5 %copy-start.8 = (s32[1,20]{1,0:T(1,128)S(1)}, s32[1,20]{1,0:T(1,128)}, u32[]{:S(2)}) copy-start(s32[1,20]{1,0:T(1,128)} %touched_hbm.9) | copy-start | bytes 244
  46.3 1.5 %copy-start = (f32[20,256,128]{2,1,0:T(8,128)}, f32[20,256,128]{2,1,0:T(8,128)S(1)}, u32[]{:S(2)}) copy-start(f32[20,256,128]{2,1,0:T(8,128)S(1)} %get-tuple-element.9.sums_ref.refs_4_) | copy-start | bytes 7864324
  47.8 3.0 %collective-permute-start.5 = (f32[8,128]{1,0:T(8,128)S(1)}, f32[8,128]{1,0:T(8,128)S(1)}, u32[]{:S(2)}, u32[]{:S(2)}) collective-permute-start(f32[8,128]{1,0:T(8,128)S(1)} %get-tuple-element.8.refs_0_), channel_id=1, source_target_pairs={{0,3},{1,2},{2,1},{3,0},{4,7},{5,6},{6,5},{7,4},{8,11},{9,10},{10,... | collective-permute-start | bytes 12296 | tf_op jit(solution)/shard_map/ppermute | solution.py:427
  47.8 3.6 %collective-permute-start.4 = (f32[8,128]{1,0:T(8,128)S(1)}, f32[8,128]{1,0:T(8,128)S(1)}, u32[]{:S(2)}, u32[]{:S(2)}) collective-permute-start(f32[8,128]{1,0:T(8,128)S(1)} %get-tuple-element.8.refs_0_), channel_id=1, source_target_pairs={{0,2},{1,3},{2,0},{3,1},{4,6},{5,7},{6,4},{7,5},{8,10},{9,11},{10,... | collective-permute-start | bytes 12296 | tf_op jit(solution)/shard_map/ppermute | solution.py:427
  48.7 2.7 %collective-permute-start.3 = (f32[8,128]{1,0:T(8,128)S(1)}, f32[8,128]{1,0:T(8,128)S(1)}, u32[]{:S(2)}, u32[]{:S(2)}) collective-permute-start(f32[8,128]{1,0:T(8,128)S(1)} %get-tuple-element.8.refs_0_), channel_id=1, source_target_pairs={{0,1},{1,0},{2,3},{3,2},{4,5},{5,4},{6,7},{7,6},{8,9},{9,8},{10,11... | collective-permute-start | bytes 12296 | tf_op jit(solution)/shard_map/ppermute | solution.py:427
  52.0 17.4 %collective-permute-start.8 = (f32[8,128]{1,0:T(8,128)}, f32[8,128]{1,0:T(8,128)}, u32[]{:S(2)}, u32[]{:S(2)}) collective-permute-start(f32[8,128]{1,0:T(8,128)} %shard_map.82.refs_0_), channel_id=1, source_target_pairs={{0,12},{1,13},{2,14},{3,15},{4,8},{5,9},{6,10},{7,11},{8,4},{9,5},... | collective-permute-start | bytes 12296 | tf_op jit(solution)/shard_map/ppermute | solution.py:427
  53.5 15.9 %collective-permute-start.7 = (f32[8,128]{1,0:T(8,128)}, f32[8,128]{1,0:T(8,128)}, u32[]{:S(2)}, u32[]{:S(2)}) collective-permute-start(f32[8,128]{1,0:T(8,128)} %shard_map.82.refs_0_), channel_id=1, source_target_pairs={{0,8},{1,9},{2,10},{3,11},{4,12},{5,13},{6,14},{7,15},{8,0},{9,1},... | collective-permute-start | bytes 12296 | tf_op jit(solution)/shard_map/ppermute | solution.py:427
  54.1 15.3 %collective-permute-start.6 = (f32[8,128]{1,0:T(8,128)}, f32[8,128]{1,0:T(8,128)}, u32[]{:S(2)}, u32[]{:S(2)}) collective-permute-start(f32[8,128]{1,0:T(8,128)} %shard_map.82.refs_0_), channel_id=1, source_target_pairs={{0,4},{1,5},{2,6},{3,7},{4,0},{5,1},{6,2},{7,3},{8,12},{9,13},{10,... | collective-permute-start | bytes 12296 | tf_op jit(solution)/shard_map/ppermute | solution.py:427
  59.0 1.5 %copy-start.3 = (f32[20,256,128]{2,1,0:T(8,128)}, f32[20,256,128]{2,1,0:T(8,128)S(1)}, u32[]{:S(2)}) copy-start(f32[20,256,128]{2,1,0:T(8,128)S(1)} %shard_map.83.refs_6_) | copy-start | bytes 7864324
  64.7 1.7 %copy-start.1 = (f32[20,256,128]{2,1,0:T(8,128)S(1)}, f32[20,256,128]{2,1,0:T(8,128)}, u32[]{:S(2)}) copy-start(f32[20,256,128]{2,1,0:T(8,128)} %copy-done) | copy-start | bytes 7864324
  66.4 0.7 copy-start.9
  67.1 2.4 %copy-start.4 = (f32[20,256,128]{2,1,0:T(8,128)S(1)}, f32[20,256,128]{2,1,0:T(8,128)}, u32[]{:S(2)}) copy-start(f32[20,256,128]{2,1,0:T(8,128)} %copy-done.3) | copy-start | bytes 7864324
  69.4 2.5 %copy-start.2 = (f32[10240,128]{1,0:T(8,128)S(1)}, f32[10240,128]{1,0:T(8,128)}, u32[]{:S(2)}) copy-start(f32[10240,128]{1,0:T(8,128)} %param.10) | copy-start | bytes 15728644
  71.9 0.8 %copy-start.6 = (f32[10240]{0:T(1024)S(1)}, f32[10240]{0:T(1024)}, u32[]{:S(2)}) copy-start(f32[10240]{0:T(1024)} %param.11) | copy-start | bytes 122884

commit v2 on v1

--- a/solution.py
+++ b/solution.py
@@ -39,45 +39,55 @@
     return jax.ShapeDtypeStruct(shape, dtype)
 
 
-def pack_kernel(slots, ids_hbm, grads_hbm, out_ref, ids_ref, sems):
-    groups = ids_ref.shape[0]
+def pack_kernel(slots, blocks_here, ids_hbm, home_hbm, grads_hbm, out_ref, ids_ref, home_ref, sems):
     fetch = pltpu.make_async_copy(ids_hbm, ids_ref, sems.at[0])
-    copy = pltpu.make_async_copy(grads_hbm, out_ref.at[:, pl.ds(0, slots), :], sems.at[1])
+    fetch_home = pltpu.make_async_copy(home_hbm, home_ref, sems.at[1])
+    copy = pltpu.make_async_copy(grads_hbm, out_ref.at[:, pl.ds(0, slots), :], sems.at[2])
     fetch.start()
+    fetch_home.start()
     copy.start()
     row = lax.broadcasted_iota(jnp.int32, (META, LANES), 0)
     fetch.wait()
-    for group in range(groups):
-        ids = jnp.broadcast_to(ids_ref[group : group + 1, :], (META, LANES))
-        top = jnp.where(ids >= 0, ids >> 16, -1)
-        digits = jnp.where(
-            row == 0, top, jnp.where(row == 1, (ids >> 8) & 255, ids & 255)
-        )
-        out_ref[group, slots : slots + META, :] = digits.astype(jnp.float32).astype(
-            jnp.bfloat16
-        )
+    fetch_home.wait()
+    ids = ids_ref[...]
+    block = ids >> 8
+    lo, hi = block & (LANES - 1), block >> 7
+    home = jnp.zeros_like(ids)
+    for r in range(home_ref.shape[0]):
+        line = jnp.broadcast_to(home_ref[r : r + 1, :], ids.shape)
+        home = jnp.where(hi == r, jnp.take_along_axis(line, lo, axis=1), home)
+    owner = lax.broadcasted_iota(jnp.int32, ids.shape, 0)
+    local = jnp.where(ids >= 0, home - owner * blocks_here, LANES - 1).astype(jnp.float32)
+    within = (ids & (BLOCK - 1)).astype(jnp.float32)
+    for group in range(ids.shape[0]):
+        here = jnp.broadcast_to(local[group : group + 1, :], row.shape)
+        there = jnp.broadcast_to(within[group : group + 1, :], row.shape)
+        digits = jnp.where(row == 0, here, there)
+        out_ref[group, slots : slots + META, :] = digits.astype(jnp.bfloat16)
     copy.wait()
 
 
-def pack(ids, grads):
+def pack(ids, home, grads, blocks_here):
     groups, slots, width = grads.shape
     pad = LANES - slots
     ids = jnp.pad(ids, ((0, 0), (0, pad)), constant_values=-1) if pad else ids
-    return call(
-        functools.partial(pack_kernel, slots),
+    assert blocks_here < LANES
+    return call(
+        functools.partial(pack_kernel, slots, blocks_here),
         1.0,
-        64,
+        63.2,
         out_shape=like((groups, slots + META, width), grads.dtype),
-        in_specs=[HBM, HBM],
+        in_specs=[HBM] * 3,
         out_specs=VMEM,
         scratch_shapes=[
             pltpu.VMEM((groups, LANES), jnp.int32),
-            pltpu.SemaphoreType.DMA((2,)),
-        ],
-    )(ids, grads)
-
-
-def keep_kernel(touched_hbm, table_hbm, out_hbm, listed, bounce, other, sems):
+            pltpu.VMEM(home.shape, jnp.int32),
+            pltpu.SemaphoreType.DMA((3,)),
+        ],
+    )(ids, home, grads)
+
+
+def keep_kernel(touched_hbm, table_hbm, out_hbm, slot_ref, listed, bounce, other, sems):
     blocks, touch = table_hbm.shape[0], touched_hbm.shape[1]
     fetch = pltpu.make_async_copy(touched_hbm, listed, sems.at[0])
     fetch.start()
@@ -89,11 +99,14 @@
     lax.fori_loop(0, blocks, clear, 0)
     fetch.wait()
 
-    def mark(t, _):
-        other[listed[0, t]] = 1
-        return 0
-
-    lax.fori_loop(0, touch, mark, 0)
+    lane = lax.broadcasted_iota(jnp.int32, slot_ref.shape, 1)
+
+    def mark(t, slot):
+        b = listed[0, t]
+        other[b] = 1
+        return jnp.where(lane == b, t, slot)
+
+    slot_ref[...] = lax.fori_loop(0, touch, mark, jnp.full(slot_ref.shape, -1, jnp.int32))
 
     def pull(b, count):
         free = other[b] == 0
@@ -123,10 +136,10 @@
     return call(
         keep_kernel,
         4.0,
-        64,
-        out_shape=like(table.shape, table.dtype),
+        60,
+        out_shape=(like(table.shape, table.dtype), like((8, LANES), jnp.int32)),
         in_specs=[HBM, HBM],
-        out_specs=HBM,
+        out_specs=(HBM, VMEM),
         scratch_shapes=[
             pltpu.SMEM((1, touch), jnp.int32),
             pltpu.VMEM((blocks - touch, BLOCK, width), table.dtype),
@@ -136,67 +149,35 @@
     )(touched, table)
 
 
-def keys_kernel(slots, blocks_here, touched_hbm, home_hbm, data_ref, keys_ref, listed, home_ref, sems):
-    a = pltpu.make_async_copy(touched_hbm, listed, sems.at[0])
-    b = pltpu.make_async_copy(home_hbm, home_ref, sems.at[1])
-    a.start()
-    b.start()
-    groups, touch = data_ref.shape[0], listed.shape[1]
+def slot_keys(slot_ref, data_ref, slots):
+    groups = data_ref.shape[0]
     per = LANES // slots
     lane = lax.broadcasted_iota(jnp.int32, (1, LANES), 1)
     meta = data_ref[:, slots : slots + META, :].astype(jnp.float32)
-    top, mid, low = (meta[:, i, :].astype(jnp.int32) for i in range(3))
-    block = top * 256 + mid
-    lo, hi = block & (LANES - 1), block >> 7
-    home = jnp.zeros_like(block)
-    a.wait()
-    b.wait()
-    for r in range(home_ref.shape[0]):
-        line = jnp.broadcast_to(home_ref[r : r + 1, :], block.shape)
-        found = jnp.take_along_axis(line, lo, axis=1)
-        home = jnp.where(hi == r, found, home)
-    local = jnp.where(top >= 0, home - lax.axis_index("shard") * blocks_here, -1)
-    keys = jnp.full_like(block, -1)
-    for t in range(touch):
-        keys = jnp.where(local == listed[0, t], t * BLOCK + low, keys)
-    if per == 1:
-        keys_ref[...] = keys
-        return
+    local, within = (meta[:, i, :].astype(jnp.int32) for i in range(2))
+    table = jnp.broadcast_to(slot_ref[0:1, :], local.shape)
+    slot = jnp.take_along_axis(table, local, axis=1)
+    keys = jnp.where(slot >= 0, slot * BLOCK + within, -1)
+    lines = []
     for g in range(groups // per):
         line = keys[g * per : g * per + 1, :]
         for j in range(1, per):
             key = pltpu.roll(keys[g * per + j : g * per + j + 1, :], j * slots, 1)
             line = jnp.where((lane >= j * slots) & (lane < (j + 1) * slots), key, line)
-        keys_ref[g : g + 1, :] = line
-
-
-def slot_keys(touched, home, data, slots, blocks_here):
-    groups = data.shape[0]
-    return call(
-        functools.partial(keys_kernel, slots, blocks_here),
-        1.0,
-        4,
-        out_shape=like((groups * slots // LANES, LANES), jnp.int32),
-        in_specs=[HBM, HBM, VMEM],
-        out_specs=VMEM,
-        scratch_shapes=[
-            pltpu.SMEM(touched.shape, jnp.int32),
-            pltpu.VMEM(home.shape, jnp.int32),
-            pltpu.SemaphoreType.DMA((2,)),
-        ],
-    )(touched, home, data)
-
-
-def add_rows(slots, fresh, squared, first, keys_ref, data_ref, *refs):
+        lines.append(line)
+    return lines
+
+
+def add_rows(slots, fresh, squared, slot_ref, data_ref, *refs):
     sums_ref, weights = refs[0 if fresh else 1], refs[-1]
     touch, _, width = sums_ref.shape
     per = TILE // slots
     tiles = data_ref.shape[0] // per
     many = next(m for m in (4, 2, 1) if touch % m == 0)
+    lines = slot_keys(slot_ref, data_ref, slots)
     key_rows = []
     for k in range(tiles):
-        at = first + 2 * k
-        pair = [keys_ref[at + i : at + i + 1, :] for i in range(2)]
+        pair = lines[2 * k : 2 * k + 2]
         upper = [((key >> 7) & 1).astype(jnp.float32) for key in pair]
         upper = [jnp.broadcast_to(u, (LANES, LANES)).T for u in upper]
         upper = jnp.concatenate(upper, axis=0).astype(jnp.bfloat16)
@@ -232,11 +213,11 @@
         refs[-2][...] = carry
 
 
-def sums_of(keys, data, slots, touch, first=0, sums=None, squared=False):
+def sums_of(slot, data, slots, touch, sums=None, squared=False):
     width = data.shape[-1]
     fresh = sums is None
     return call(
-        functools.partial(add_rows, slots, fresh, squared, first),
+        functools.partial(add_rows, slots, fresh, squared),
         data.shape[0] * slots / 512,
         10,
         out_shape=(like((touch, BLOCK, width)), like((8, width)))[: 1 + squared],
@@ -246,7 +227,7 @@
             pltpu.VMEM((data.shape[0] * slots // TILE, TILE, 2 * width), data.dtype)
         ],
         input_output_aliases={} if fresh else {2: 0},
-    )(keys, data, *([] if fresh else [sums]))
+    )(slot, data, *([] if fresh else [sums]))
 
 
 def spread_kernel(touched_hbm, accum_hbm, rep_ref, listed, accum, sems):
@@ -348,17 +329,19 @@
 
 
 def update_kernel(limit, touched_hbm, *refs):
-    out_hbm, new_accum_ref, fresh, listed, sems = refs[-5:]
-    sums_ref, table_ref, accum_rep_ref, mean_rep_ref, accum_ref, mean_ref = refs[-12:-6]
+    out_hbm, new_accum_hbm, fresh, new_accum, listed, sems = refs[-6:]
+    sums_ref, table_ref, accum_rep_ref, mean_rep_ref, accum_ref, mean_ref = refs[-13:-7]
     fetch = pltpu.make_async_copy(touched_hbm, listed, sems.at[0])
     fetch.start()
     square = refs[0][...]
-    for ref in refs[1:-12]:
+    for ref in refs[1:-13]:
         square = square + ref[...]
     square = jnp.sum(jnp.sum(square, axis=1, keepdims=True), axis=0, keepdims=True)
     factor = limit / jnp.maximum(jnp.sqrt(square), limit)
     factor_sq = factor * factor
-    new_accum_ref[...] = accum_ref[...] + factor_sq * mean_ref[...]
+    new_accum[...] = accum_ref[...] + factor_sq * mean_ref[...]
+    put = pltpu.make_async_copy(new_accum, new_accum_hbm, sems.at[2])
+    put.start()
     rate = LEARN_RATE * factor
     fetch.wait()
 
@@ -370,6 +353,7 @@
         return 0
 
     lax.fori_loop(0, fresh.shape[0], step, 0)
+    put.wait()
     pltpu.make_async_copy(fresh, fresh, sems.at[1]).wait()
 
 
@@ -381,11 +365,12 @@
         8,
         out_shape=(like(table.shape, table.dtype), like(accum.shape, accum.dtype)),
         in_specs=[HBM] + [VMEM] * (n + 6) + [HBM],
-        out_specs=(HBM, VMEM),
+        out_specs=(HBM, HBM),
         scratch_shapes=[
             pltpu.VMEM(sums.shape, table.dtype),
+            pltpu.VMEM(accum.shape, accum.dtype),
             pltpu.SMEM(touched.shape, jnp.int32),
-            pltpu.SemaphoreType.DMA((2,)),
+            pltpu.SemaphoreType.DMA((3,)),
         ],
         input_output_aliases={n + 7: 0},
     )(touched, *squares, sums, old, accum_rep, mean_rep, accum, mean, table)
@@ -404,19 +389,16 @@
     accum = row_accum.reshape(-1, LANES)
     home = jnp.pad(block_home, (0, -block_home.shape[0] % LANES)).reshape(-1, LANES)
 
-    data = pack(ids, grads)
+    data = pack(ids, home, grads, blocks_here)
     data = lax.all_to_all(data, "shard", 0, 0, tiled=True)
-    table_out = keep_untouched(touched, table)
+    table_out, slot = keep_untouched(touched, table)
     split = shards // 2
     other_a = lax.ppermute(data[:split], "rep", swap)
     other_b = lax.ppermute(data[split:], "rep", swap)
-    keys = slot_keys(touched, home, data, slots, blocks_here)
-    other_keys = lax.ppermute(keys, "rep", swap)
-    (sums,) = sums_of(keys, data, slots, touch)
+    (sums,) = sums_of(slot, data, slots, touch)
     accum_rep = spread_accum(touched, accum)
-    (sums,) = sums_of(other_keys, other_a, slots, touch, 0, sums)
-    first = split * slots // LANES
-    sums, square = sums_of(other_keys, other_b, slots, touch, first, sums, True)
+    (sums,) = sums_of(slot, other_a, slots, touch, sums)
+    sums, square = sums_of(slot, other_b, slots, touch, sums, True)
     squares = [square]
     stride = 1
     while stride < shards:
@@ -429,7 +411,7 @@
             )
             for r in range(1, fan)
         ]
-        stride *= fan
+        stride = stride * fan
     mean_rep, mean = row_means(touched, sums, accum.shape[0])
     table_out, accum_out = update(
         limit, touched, squares, sums, table, accum_rep, mean_rep, accum, mean, table_out

time: 76.6 us -> 59.5 us (0.78)
  local copies, waits for them, and re-layouts: 10.1 us -> 0.75 us
  waiting for transfers between devices: 7.1 us -> 2.67 us
  Pallas kernels: 24.2 us -> 22.4 us
  starting transfers between devices: 9.92 us -> 8.46 us
    unnamed x22 -> x10, local copies, waits for them, and re-layouts: 10 us -> 0.71 us
    ppermute x1 -> x0, waiting for transfers between devices: 5.33 us -> none  [step(): other_keys = lax.ppermute(keys, 'rep', swap)]
    ppermute x1 -> x0, starting transfers between devices: 1.58 us -> none  [step(): other_keys = lax.ppermute(keys, 'rep', swap)]
    pallas_call x1, Pallas kernels: 3.41 us -> 2.11 us  [update(): call(functools.partial(update_kernel, limit), 2.5, 8, out_shape=(like(tab...]
    ppermute x1, waiting for transfers between devices: 0.01 us -> 0.84 us  [step(): other_b = lax.ppermute(data[split:], 'rep', swap)]
    pallas_call x6 -> x5, Pallas kernels: 15.3 us -> 15.4 us  [the longest x3 8.75 us: sums_of(): call(functools.partial(add_rows, slots, fresh, squared), data.shape[0] *...]
  transfers between devices with their start and end apart: 9 -> 8, of which waited for: 3 -> 3; matrix products, arithmetic and copies ran while one was open for 0% -> 0% of each run, Pallas kernels for 21% -> 27%
where the time goes in v2:
time: 59.5 us; the launch traced here: 59.1 us
  blocking collectives  24.1 us (41%)
  Pallas kernels  22.4 us (38%)
  starting transfers between devices  8.46 us (14%)
  waiting for transfers between devices  2.67 us (4%)
  between operations  0.8 us (1%)
  local copies, waits for them, and re-layouts  0.75 us (1%)
    all_to_all x1, blocking collectives, step(): data = lax.all_to_all(data, 'shard', 0, 0, tiled=True)  24.1 us
    pallas_call x3, Pallas kernels, sums_of(): call(functools.partial(add_rows, slots, fresh, squared), data.shape[0] *...  8.75 us
    ppermute x6, starting transfers between devices, step(): lax.ppermute(squares[0], 'shard', [(i, i ^ r * stride) for i in range(sha...  6.37 us
    pallas_call x1, Pallas kernels, keep_untouched(): call(keep_kernel, 4.0, 60, out_shape=(like(table.shape, table.dtype), lik...  4.71 us
    pallas_call x1, Pallas kernels, spread_accum(): call(spread_kernel, 2.0, 8, out_shape=like((touch, BLOCK, LANES)), in_spe...  2.57 us
    pallas_call x1, Pallas kernels, row_means(): call(means_kernel, 2.0, 8, out_shape=(like((touch, BLOCK, LANES)), like((...  2.33 us
    pallas_call x1, Pallas kernels, update(): call(functools.partial(update_kernel, limit), 2.5, 8, out_shape=(like(tab...  2.11 us
    pallas_call x1, Pallas kernels, pack(): call(functools.partial(pack_kernel, slots, blocks_here), 1.0, 63.2, out_s...  1.9 us
  transfers between devices with their start and end apart: 8, of which 3 were waited for; matrix products, arithmetic and copies ran while one was open for 0% of the time, Pallas kernels for 27%

profile of v2, /device:TPU:0, one launch (start us, length us, event | category | flops | bytes accessed | tf_op | source)
XLA Modules:
  0.0 59.1 jit_solution(11562283223340386703)
XLA Ops:
  0.6 1.9 %shard_map.78 = bf16[16,136,128]{2,1,0:T(8,128)(2,1)} custom-call(s32[16,128]{1,0:T(8,128)} %bitcast.15, s32[5,128]{1,0:T(8,128)} %bitcast.16, bf16[16,128,128]{2,1,0:T(8,128)(2,1)} %bitcast.14), custom_call_target="tpu_custom_call" | custom-call | flops 4000000 | bytes 1048576 | tf_op jit(solution)/shard_map/pallas_call | solution.py:75
  2.5 24.1 %all_to_all.5.data_ref = bf16[16,136,128]{2,1,0:T(8,128)(2,1)S(1)} all-to-all(bf16[16,136,128]{2,1,0:T(8,128)(2,1)} %shard_map.78), channel_id=1, replica_groups=mesh['rep'=2,'shard'=16] {'shard'}, dimensions={0} | all-to-all | bytes 1114112 | tf_op jit(solution)/shard_map/all_to_all | solution.py:393
  26.7 1.6 %collective-permute-start.1 = (bf16[8,136,128]{2,1,0:T(8,128)(2,1)S(1)}, bf16[8,136,128]{2,1,0:T(8,128)(2,1)S(1)}, u32[]{:S(2)}, u32[]{:S(2)}) collective-permute-start(bf16[8,136,128]{2,1,0:T(8,128)(2,1)S(1)} %get-tuple-element.18), channel_id=1, source_target_pairs={{0,16},{16,0},{1,17},{17,1},{2,18},{18,2},{3,19},{19,3},{4,20},{20... | collective-permute-start | bytes 835592 | tf_op jit(solution)/shard_map/ppermute | solution.py:396
  28.2 0.5 collective-permute-start
  28.8 4.7 %shard_map.77 = (f32[40,256,128]{2,1,0:T(8,128)}, s32[8,128]{1,0:T(8,128)}) custom-call(s32[1,20]{1,0:T(1,128)} %touched_hbm.7, f32[40,256,128]{2,1,0:T(8,128)} %bitcast.7), custom_call_target="tpu_custom_call" | custom-call | flops 16000000 | bytes 1048576 | tf_op jit(solution)/shard_map/pallas_call | solution.py:136
  33.5 0.0 copy-start.1
  33.5 0.7 %copy-done.1 = s32[8,128]{1,0:T(8,128)S(1)} copy-done((s32[8,128]{1,0:T(8,128)S(1)}, s32[8,128]{1,0:T(8,128)}, u32[]{:S(2)}) %copy-start.1) | copy-done | bytes 4120
  34.2 3.9 %shard_map.79.refs_0_ = f32[20,256,128]{2,1,0:T(8,128)S(1)} custom-call(s32[8,128]{1,0:T(8,128)S(1)} %copy-done.1, bf16[16,136,128]{2,1,0:T(8,128)(2,1)S(1)} %all_to_all.5.data_ref), custom_call_target="tpu_custom_call" | custom-call | flops 16000000 | bytes 1048576 | tf_op jit(solution)/shard_map/pallas_call | solution.py:219
  38.0 0.0 collective-permute-done.1.data_ref
  38.0 0.0 slice-start
  38.0 2.4 %shard_map.80.refs_0_ = f32[20,256,128]{2,1,0:T(8,128)S(1)} custom-call(s32[8,128]{1,0:T(8,128)S(1)} %copy-done.1, bf16[8,136,128]{2,1,0:T(8,128)(2,1)S(1)} %collective-permute-done.1.data_ref, f32[20,256,128]{2,1,0:T(8,128)S(1)} %shard_map.79.refs_0_), custom_call_target="tpu_custom_call", output_to_operand_aliasing={{}: (2, {})} | custom-call | flops 8000000 | bytes 1048576 | tf_op jit(solution)/shard_map/pallas_call | solution.py:219
  40.5 0.0 copy-start
  40.5 0.0 copy-start.2
  40.5 0.0 slice-start.1
  40.5 0.8 %collective-permute-done.data_ref = bf16[8,136,128]{2,1,0:T(8,128)(2,1)S(1)} collective-permute-done((bf16[8,136,128]{2,1,0:T(8,128)(2,1)S(1)}, bf16[8,136,128]{2,1,0:T(8,128)(2,1)S(1)}, u32[]{:S(2)}, u32[]{:S(2)}) %collective-permute-start) | collective-permute-done | bytes 278560 | tf_op jit(solution)/shard_map/ppermute | solution.py:397
  41.4 2.5 %shard_map.81 = (f32[20,256,128]{2,1,0:T(8,128)S(1)}, f32[8,128]{1,0:T(8,128)S(1)}) custom-call(s32[8,128]{1,0:T(8,128)S(1)} %copy-done.1, bf16[8,136,128]{2,1,0:T(8,128)(2,1)S(1)} %collective-permute-done.data_ref, f32[20,256,128]{2,1,0:T(8,128)S(1)} %shard_map.80.refs_0_), custom_call_target="tpu_custom_call", output_to_operand_aliasing={{0}: (2, {})} | custom-call | flops 8000000 | bytes 1048576 | tf_op jit(solution)/shard_map/pallas_call | solution.py:219
  43.8 0.1 collective-permute-start.4
  43.9 0.9 %collective-permute-start.3 = (f32[8,128]{1,0:T(8,128)S(1)}, f32[8,128]{1,0:T(8,128)S(1)}, u32[]{:S(2)}, u32[]{:S(2)}) collective-permute-start(f32[8,128]{1,0:T(8,128)S(1)} %get-tuple-element.11.refs_0_), channel_id=1, source_target_pairs={{0,2},{1,3},{2,0},{3,1},{4,6},{5,7},{6,4},{7,5},{8,10},{9,11},{10,... | collective-permute-start | bytes 12296 | tf_op jit(solution)/shard_map/ppermute | solution.py:409
  44.8 1.0 %collective-permute-start.2 = (f32[8,128]{1,0:T(8,128)S(1)}, f32[8,128]{1,0:T(8,128)S(1)}, u32[]{:S(2)}, u32[]{:S(2)}) collective-permute-start(f32[8,128]{1,0:T(8,128)S(1)} %get-tuple-element.11.refs_0_), channel_id=1, source_target_pairs={{0,1},{1,0},{2,3},{3,2},{4,5},{5,4},{6,7},{7,6},{8,9},{9,8},{10,11... | collective-permute-start | bytes 12296 | tf_op jit(solution)/shard_map/ppermute | solution.py:409
  45.8 1.2 %collective-permute-done.4.refs_3_ = f32[8,128]{1,0:T(8,128)S(1)} collective-permute-done((f32[8,128]{1,0:T(8,128)S(1)}, f32[8,128]{1,0:T(8,128)S(1)}, u32[]{:S(2)}, u32[]{:S(2)}) %collective-permute-start.4) | collective-permute-done | bytes 4128 | tf_op jit(solution)/shard_map/ppermute | solution.py:409
  46.9 0.7 %collective-permute-done.3.refs_2_ = f32[8,128]{1,0:T(8,128)S(1)} collective-permute-done((f32[8,128]{1,0:T(8,128)S(1)}, f32[8,128]{1,0:T(8,128)S(1)}, u32[]{:S(2)}, u32[]{:S(2)}) %collective-permute-start.3) | collective-permute-done | bytes 4128 | tf_op jit(solution)/shard_map/ppermute | solution.py:409
  47.6 0.0 collective-permute-done.2.refs_1_
  47.6 1.5 %collective-permute-start.7 = (f32[8,128]{1,0:T(8,128)S(1)}, f32[8,128]{1,0:T(8,128)S(1)}, u32[]{:S(2)}, u32[]{:S(2)}) collective-permute-start(f32[8,128]{1,0:T(8,128)S(1)} %shard_map.82.refs_0_), channel_id=1, source_target_pairs={{0,12},{1,13},{2,14},{3,15},{4,8},{5,9},{6,10},{7,11},{8,4},{9,5},... | collective-permute-start | bytes 12296 | tf_op jit(solution)/shard_map/ppermute | solution.py:409
  49.1 0.6 collective-permute-start.6
  49.7 2.3 %collective-permute-start.5 = (f32[8,128]{1,0:T(8,128)S(1)}, f32[8,128]{1,0:T(8,128)S(1)}, u32[]{:S(2)}, u32[]{:S(2)}) collective-permute-start(f32[8,128]{1,0:T(8,128)S(1)} %shard_map.82.refs_0_), channel_id=1, source_target_pairs={{0,4},{1,5},{2,6},{3,7},{4,0},{5,1},{6,2},{7,3},{8,12},{9,13},{10,... | collective-permute-start | bytes 12296 | tf_op jit(solution)/shard_map/ppermute | solution.py:409
  52.1 0.0 copy-done
  52.1 0.0 copy-done.2
  52.1 2.6 %shard_map.83.refs_6_ = f32[20,256,128]{2,1,0:T(8,128)S(1)} custom-call(s32[1,20]{1,0:T(1,128)S(1)} %copy-done.2, f32[80,128]{1,0:T(8,128)S(1)} %bitcast.11), custom_call_target="tpu_custom_call" | custom-call | flops 8000000 | bytes 1048576 | tf_op jit(solution)/shard_map/pallas_call | solution.py:254
  54.6 2.3 %shard_map.84 = (f32[20,256,128]{2,1,0:T(8,128)S(1)}, f32[80,128]{1,0:T(8,128)S(1)}) custom-call(s32[1,20]{1,0:T(1,128)S(1)} %copy-done.2, f32[20,256,128]{2,1,0:T(8,128)S(1)} %get-tuple-element.12.sums_ref.refs_4_), custom_call_target="tpu_custom_call" | custom-call | flops 8000000 | bytes 1048576 | tf_op jit(solution)/shard_map/pallas_call | solution.py:298
  57.0 0.0 collective-permute-done.7.refs_3_
  57.0 0.0 collective-permute-done.6.refs_2_
  57.0 0.0 collective-permute-done.5.refs_1_
  57.0 0.0 slice-done
  57.0 0.0 slice-done.1
  57.0 2.1 %shard_map.85 = (f32[40,256,128]{2,1,0:T(8,128)}, f32[80,128]{1,0:T(8,128)}) custom-call(s32[1,20]{1,0:T(1,128)S(1)} %copy-done.2, f32[8,128]{1,0:T(8,128)S(1)} %shard_map.82.refs_0_, f32[8,128]{1,0:T(8,128)S(1)} %collective-permute-done.5.refs_1_, f32[8,128]{1,0:T(8,128)S(1)} %collective-permute-done.6.refs_2_, ...), custom_call_target="tpu_custom_call", output_to_operand_aliasing={{0}: (11, {})} | custom-call | flops 10000000 | bytes 1048576 | tf_op jit(solution)/shard_map/pallas_call | solution.py:362
  (3 shorter events, 0.0 us)
Async XLA Ops:
  26.7 11.4 %collective-permute-start.1 = (bf16[8,136,128]{2,1,0:T(8,128)(2,1)S(1)}, bf16[8,136,128]{2,1,0:T(8,128)(2,1)S(1)}, u32[]{:S(2)}, u32[]{:S(2)}) collective-permute-start(bf16[8,136,128]{2,1,0:T(8,128)(2,1)S(1)} %get-tuple-element.18), channel_id=1, source_target_pairs={{0,16},{16,0},{1,17},{17,1},{2,18},{18,2},{3,19},{19,3},{4,20},{20... | collective-permute-start | bytes 835592 | tf_op jit(solution)/shard_map/ppermute | solution.py:396
  28.2 13.1 %collective-permute-start = (bf16[8,136,128]{2,1,0:T(8,128)(2,1)S(1)}, bf16[8,136,128]{2,1,0:T(8,128)(2,1)S(1)}, u32[]{:S(2)}, u32[]{:S(2)}) collective-permute-start(bf16[8,136,128]{2,1,0:T(8,128)(2,1)S(1)} %get-tuple-element.19), channel_id=1, source_target_pairs={{0,16},{16,0},{1,17},{17,1},{2,18},{18,2},{3,19},{19,3},{4,20},{20... | collective-permute-start | bytes 835592 | tf_op jit(solution)/shard_map/ppermute | solution.py:397
  33.5 0.7 %copy-start.1 = (s32[8,128]{1,0:T(8,128)S(1)}, s32[8,128]{1,0:T(8,128)}, u32[]{:S(2)}) copy-start(s32[8,128]{1,0:T(8,128)} %get-tuple-element.10.slot_ref) | copy-start | bytes 12292
  38.0 19.0 %slice-start = ((s8[5242880]{0:T(1024)(128)(4,1)}), s8[4194304]{0:T(1024)(128)(4,1)S(1)}, s32[]{:S(2)}) async-start(s8[5242880]{0:T(1024)(128)(4,1)} %bitcast.8), calls=%async_computation.1 | async-start | bytes 8388608
  40.5 11.6 %copy-start = (f32[10240]{0:T(1024)S(1)}, f32[10240]{0:T(1024)}, u32[]{:S(2)}) copy-start(f32[10240]{0:T(1024)} %param.11) | copy-start | bytes 122884
  40.5 11.6 %copy-start.2 = (s32[1,20]{1,0:T(1,128)S(1)}, s32[1,20]{1,0:T(1,128)}, u32[]{:S(2)}) copy-start(s32[1,20]{1,0:T(1,128)} %touched_hbm.7) | copy-start | bytes 244
  40.5 16.5 %slice-start.1 = ((s8[5242880]{0:T(1024)(128)(4,1)}), s8[1048576]{0:T(1024)(128)(4,1)S(1)}, s32[]{:S(2)}) async-start(s8[5242880]{0:T(1024)(128)(4,1)} %bitcast.8), calls=%async_computation.2 | async-start | bytes 2097152
  43.8 3.1 %collective-permute-start.4 = (f32[8,128]{1,0:T(8,128)S(1)}, f32[8,128]{1,0:T(8,128)S(1)}, u32[]{:S(2)}, u32[]{:S(2)}) collective-permute-start(f32[8,128]{1,0:T(8,128)S(1)} %get-tuple-element.11.refs_0_), channel_id=1, source_target_pairs={{0,3},{1,2},{2,1},{3,0},{4,7},{5,6},{6,5},{7,4},{8,11},{9,10},{10,... | collective-permute-start | bytes 12296 | tf_op jit(solution)/shard_map/ppermute | solution.py:409
  43.9 3.7 %collective-permute-start.3 = (f32[8,128]{1,0:T(8,128)S(1)}, f32[8,128]{1,0:T(8,128)S(1)}, u32[]{:S(2)}, u32[]{:S(2)}) collective-permute-start(f32[8,128]{1,0:T(8,128)S(1)} %get-tuple-element.11.refs_0_), channel_id=1, source_target_pairs={{0,2},{1,3},{2,0},{3,1},{4,6},{5,7},{6,4},{7,5},{8,10},{9,11},{10,... | collective-permute-start | bytes 12296 | tf_op jit(solution)/shard_map/ppermute | solution.py:409
  44.8 2.8 %collective-permute-start.2 = (f32[8,128]{1,0:T(8,128)S(1)}, f32[8,128]{1,0:T(8,128)S(1)}, u32[]{:S(2)}, u32[]{:S(2)}) collective-permute-start(f32[8,128]{1,0:T(8,128)S(1)} %get-tuple-element.11.refs_0_), channel_id=1, source_target_pairs={{0,1},{1,0},{2,3},{3,2},{4,5},{5,4},{6,7},{7,6},{8,9},{9,8},{10,11... | collective-permute-start | bytes 12296 | tf_op jit(solution)/shard_map/ppermute | solution.py:409
  47.6 9.4 %collective-permute-start.7 = (f32[8,128]{1,0:T(8,128)S(1)}, f32[8,128]{1,0:T(8,128)S(1)}, u32[]{:S(2)}, u32[]{:S(2)}) collective-permute-start(f32[8,128]{1,0:T(8,128)S(1)} %shard_map.82.refs_0_), channel_id=1, source_target_pairs={{0,12},{1,13},{2,14},{3,15},{4,8},{5,9},{6,10},{7,11},{8,4},{9,5},... | collective-permute-start | bytes 12296 | tf_op jit(solution)/shard_map/ppermute | solution.py:409
  49.1 7.8 %collective-permute-start.6 = (f32[8,128]{1,0:T(8,128)S(1)}, f32[8,128]{1,0:T(8,128)S(1)}, u32[]{:S(2)}, u32[]{:S(2)}) collective-permute-start(f32[8,128]{1,0:T(8,128)S(1)} %shard_map.82.refs_0_), channel_id=1, source_target_pairs={{0,8},{1,9},{2,10},{3,11},{4,12},{5,13},{6,14},{7,15},{8,0},{9,1},... | collective-permute-start | bytes 12296 | tf_op jit(solution)/shard_map/ppermute | solution.py:409
  49.7 7.3 %collective-permute-start.5 = (f32[8,128]{1,0:T(8,128)S(1)}, f32[8,128]{1,0:T(8,128)S(1)}, u32[]{:S(2)}, u32[]{:S(2)}) collective-permute-start(f32[8,128]{1,0:T(8,128)S(1)} %shard_map.82.refs_0_), channel_id=1, source_target_pairs={{0,4},{1,5},{2,6},{3,7},{4,0},{5,1},{6,2},{7,3},{8,12},{9,13},{10,... | collective-permute-start | bytes 12296 | tf_op jit(solution)/shard_map/ppermute | solution.py:409

commit v3 on v2

v3 whole, which is shorter than its diff:
```python
import functools
import math

import jax
import jax.numpy as jnp
from jax import lax
from jax.experimental import pallas as pl
from jax.experimental.pallas import tpu as pltpu
from jax.sharding import PartitionSpec as P

BLOCK = 256
CLIP_RMS = 0.25
LEARN_RATE = 0.1
DECAY_RATE = 0.05
LANES = 128
META = 8
PARTS = BLOCK // LANES
TILE = 2 * LANES
MIB = 1 << 20
WHOLE = 67043328


VMEM = pl.BlockSpec(memory_space=pltpu.VMEM)
HBM = pl.BlockSpec(memory_space=pltpu.HBM)

EARLY = 4


def call(kernel, us, mib, **kwargs):
    return pl.pallas_call(
        kernel,
        compiler_params=pltpu.CompilerParams(vmem_limit_bytes=int(min(mib * MIB, WHOLE))),
        cost_estimate=pl.CostEstimate(
            flops=int(us * 4e6), bytes_accessed=MIB, transcendentals=0
        ),
        **kwargs,
    )


def like(shape, dtype=jnp.float32):
    return jax.ShapeDtypeStruct(shape, dtype)


def pack_kernel(slots, blocks_here, ids_hbm, home_hbm, grads_hbm, out_ref, *rest):
    early, (ids_ref, home_ref, digits_ref, sems) = rest[:-4], rest[-4:]
    fetch = pltpu.make_async_copy(ids_hbm, ids_ref, sems.at[0])
    fetch_home = pltpu.make_async_copy(home_hbm, home_ref, sems.at[1])
    copy = pltpu.make_async_copy(grads_hbm, out_ref.at[:, pl.ds(0, slots), :], sems.at[2])
    fetch.start()
    fetch_home.start()
    copy.start()
    me = lax.axis_index("shard")
    copies = [
        pltpu.make_async_copy(
            grads_hbm.at[me ^ r], early[r].at[0, pl.ds(0, slots), :], sems.at[3 + r]
        )
        for r in range(len(early))
    ]
    for each in copies:
        each.start()
    row = lax.broadcasted_iota(jnp.int32, (META, LANES), 0)
    fetch.wait()
    fetch_home.wait()
    ids = ids_ref[...]
    block = ids >> 8
    lo, hi = block & (LANES - 1), block >> 7
    home = jnp.zeros_like(ids)
    for r in range(home_ref.shape[0]):
        line = jnp.broadcast_to(home_ref[r : r + 1, :], ids.shape)
        home = jnp.where(hi == r, jnp.take_along_axis(line, lo, axis=1), home)
    owner = lax.broadcasted_iota(jnp.int32, ids.shape, 0)
    local = jnp.where(ids >= 0, home - owner * blocks_here, LANES - 1).astype(jnp.float32)
    within = (ids & (BLOCK - 1)).astype(jnp.float32)
    for group in range(ids.shape[0]):
        here = jnp.broadcast_to(local[group : group + 1, :], row.shape)
        there = jnp.broadcast_to(within[group : group + 1, :], row.shape)
        digits = jnp.where(row == 0, here, there)
        out_ref[group, slots : slots + META, :] = digits.astype(jnp.bfloat16)
        digits_ref[group] = digits
    for r, ref in enumerate(early):
        ref[0, slots : slots + META, :] = digits_ref[me ^ r].astype(jnp.bfloat16)
    for each in copies:
        each.wait()
    copy.wait()


def pack(ids, home, grads, blocks_here, early):
    groups, slots, width = grads.shape
    pad = LANES - slots
    ids = jnp.pad(ids, ((0, 0), (0, pad)), constant_values=-1) if pad else ids
    assert blocks_here < LANES
    slab = (slots + META, width)
    return call(
        functools.partial(pack_kernel, slots, blocks_here),
        1.0,
        62.9,
        out_shape=(like((groups, *slab), grads.dtype),)
        + (like((1, *slab), grads.dtype),) * early,
        in_specs=[HBM] * 3,
        out_specs=(VMEM,) * (1 + early),
        scratch_shapes=[
            pltpu.VMEM((groups, LANES), jnp.int32),
            pltpu.VMEM(home.shape, jnp.int32),
            pltpu.VMEM((groups, META, LANES), jnp.float32),
            pltpu.SemaphoreType.DMA((3 + early,)),
        ],
    )(ids, home, grads)


def pick_kernel(group, data_ref, first_ref, second_ref):
    groups = data_ref.shape[0] // group
    mine = lax.axis_index("shard") // group
    first = first_ref.shape[0]
    for j in range(group, groups * group):
        where = lax.rem(mine + j // group, groups) * group + j % group
        at = j - group
        if at < first:
            first_ref[at] = data_ref[where]
        else:
            second_ref[at - first] = data_ref[where]


def pick_far(data, group):
    groups, *slab = data.shape
    last = (groups - group) // 3
    return call(
        functools.partial(pick_kernel, group),
        0.5,
        4,
        out_shape=(
            like((groups - group - last, *slab), data.dtype),
            like((last, *slab), data.dtype),
        ),
        in_specs=[VMEM],
        out_specs=(VMEM, VMEM),
    )(data)


def keep_kernel(touched_hbm, table_hbm, out_hbm, slot_ref, listed, bounce, other, sems):
    blocks, touch = table_hbm.shape[0], touched_hbm.shape[1]
    fetch = pltpu.make_async_copy(touched_hbm, listed, sems.at[0])
    fetch.start()

    def clear(b, _):
        other[b] = 0
        return 0

    lax.fori_loop(0, blocks, clear, 0)
    fetch.wait()

    lane = lax.broadcasted_iota(jnp.int32, slot_ref.shape, 1)

    def mark(t, slot):
        b = listed[0, t]
        other[b] = 1
        return jnp.where(lane == b, t, slot)

    slot_ref[...] = lax.fori_loop(0, touch, mark, jnp.full(slot_ref.shape, -1, jnp.int32))

    def pull(b, count):
        free = other[b] == 0

        @pl.when(free)
        def _():
            pltpu.make_async_copy(table_hbm.at[b], bounce.at[count], sems.at[1]).start()
            other[blocks + count] = b

        return count + free.astype(jnp.int32)

    lax.fori_loop(0, blocks, pull, 0)
    pltpu.make_async_copy(bounce, bounce, sems.at[1]).wait()

    def put(j, _):
        b = other[blocks + j]
        pltpu.make_async_copy(bounce.at[j], out_hbm.at[b], sems.at[2]).start()
        return 0

    lax.fori_loop(0, blocks - touch, put, 0)
    pltpu.make_async_copy(bounce, bounce, sems.at[2]).wait()


def keep_untouched(touched, table):
    blocks, _, width = table.shape
    touch = touched.shape[1]
    return call(
        keep_kernel,
        4.0,
        60,
        out_shape=(like(table.shape, table.dtype), like((8, LANES), jnp.int32)),
        in_specs=[HBM, HBM],
        out_specs=(HBM, VMEM),
        scratch_shapes=[
            pltpu.SMEM((1, touch), jnp.int32),
            pltpu.VMEM((blocks - touch, BLOCK, width), table.dtype),
            pltpu.SMEM((2 * blocks,), jnp.int32),
            pltpu.SemaphoreType.DMA((3,)),
        ],
    )(touched, table)


def slot_keys(slot_ref, slabs, slots):
    per = LANES // slots
    lane = lax.broadcasted_iota(jnp.int32, (1, LANES), 1)
    table = jnp.broadcast_to(slot_ref[0:1, :], (META, LANES))
    keys = []
    for ref, i in slabs:
        meta = ref[i, slots : slots + META, :].astype(jnp.float32).astype(jnp.int32)
        local = jnp.broadcast_to(meta[0:1, :], (META, LANES))
        slot = jnp.take_along_axis(table, local, axis=1)[0:1, :]
        keys.append(jnp.where(slot >= 0, slot * BLOCK + meta[1:2, :], -1))
    lines = []
    for g in range(len(slabs) // per):
        line = keys[g * per]
        for j in range(1, per):
            key = pltpu.roll(keys[g * per + j], j * slots, 1)
            line = jnp.where((lane >= j * slots) & (lane < (j + 1) * slots), key, line)
        lines.append(line)
    return lines


def add_rows(slots, count, fresh, last, slot_ref, *refs):
    data, refs = refs[:count], refs[count:]
    sums_ref, weights = refs[0 if fresh else 1], refs[-1]
    touch, _, width = sums_ref.shape
    per = TILE // slots
    slabs = [(ref, i) for ref in data for i in range(ref.shape[0])]
    tiles = len(slabs) // per
    many = next(m for m in (4, 2, 1) if touch % m == 0)
    lines = slot_keys(slot_ref, slabs, slots)
    key_rows = []
    for k in range(tiles):
        pair = lines[2 * k : 2 * k + 2]
        upper = [((key >> 7) & 1).astype(jnp.float32) for key in pair]
        upper = [jnp.broadcast_to(u, (LANES, LANES)).T for u in upper]
        upper = jnp.concatenate(upper, axis=0).astype(jnp.bfloat16)
        rows = [ref[i, 0:slots, :] for ref, i in slabs[k * per : (k + 1) * per]]
        rows = jnp.concatenate(rows, axis=0)
        high = rows * upper
        weights[k, :, width : 2 * width] = high
        weights[k, :, 0:width] = rows - high
        flat = [jnp.where(key >= 0, (key >> 8) * LANES + (key & (LANES - 1)), -1) for key in pair]
        key_rows.append(jnp.concatenate(flat, axis=1))
    row = lax.broadcasted_iota(jnp.int32, (many * LANES, TILE), 0)
    lane = lax.broadcasted_iota(jnp.int32, (LANES, LANES), 1)
    if last:
        mean_rep_ref, gathered_ref, square_ref = refs[2:5]
        gathered_ref[...] = jnp.zeros_like(gathered_ref)

    def step(u, carry):
        total = None
        for k in range(tiles):
            match = row == jnp.broadcast_to(key_rows[k] - u * (many * LANES), row.shape)
            onehot = jnp.where(match, 1.0, 0.0).astype(jnp.bfloat16)
            part = jnp.dot(onehot, weights[k], preferred_element_type=jnp.float32)
            total = part if total is None else total + part
        for i in range(many):
            t = u * many + i
            for p in range(PARTS):
                piece = total[i * LANES : (i + 1) * LANES, p * width : (p + 1) * width]
                at = pl.ds(p * LANES, LANES)
                piece = piece if fresh else piece + sums_ref[t, at, :]
                sums_ref[t, at, :] = piece
                if last:
                    mean = jnp.sum(piece * piece, axis=1, keepdims=True) * (1.0 / width)
                    mean = jnp.broadcast_to(mean, (LANES, LANES))
                    mean_rep_ref[t, at, :] = mean
                    gathered_ref[...] = jnp.where(
                        lane == t * PARTS + p, mean, gathered_ref[...]
                    )
        return carry

    lax.fori_loop(0, touch // many, step, 0)
    if last:
        square = jnp.sum(gathered_ref[...].reshape(-1, 8, LANES), axis=0) * width
        for i in range(square_ref.shape[0]):
            square_ref[i] = square


def sums_of(slot, data, slots, touch, sums=None, shards=0):
    width = data[0].shape[-1]
    count = len(data)
    slabs = sum(each.shape[0] for each in data)
    fresh, last = sums is None, shards > 0
    assert slabs * slots % TILE == 0 and touch * PARTS <= LANES
    outs = (like((touch, BLOCK, width)),)
    if last:
        outs += (like((touch, BLOCK, LANES)), like((LANES, LANES)), like((shards, 8, LANES)))
    return call(
        functools.partial(add_rows, slots, count, fresh, last),
        slabs * slots / 512,
        10,
        out_shape=outs,
        in_specs=[VMEM] * (1 + count + (not fresh)),
        out_specs=(VMEM,) * len(outs),
        scratch_shapes=[pltpu.VMEM((slabs * slots // TILE, TILE, 2 * width), data[0].dtype)],
        input_output_aliases={} if fresh else {1 + count: 0},
    )(slot, *data, *([] if fresh else [sums]))


def spread_kernel(touched_hbm, accum_hbm, rep_ref, listed, accum, sems):
    a = pltpu.make_async_copy(touched_hbm, listed, sems.at[0])
    b = pltpu.make_async_copy(accum_hbm, accum, sems.at[1])
    a.start()
    b.start()
    a.wait()
    b.wait()

    def step(t, _):
        for part in range(PARTS):
            row = accum[pl.ds(listed[0, t] * PARTS + part, 1), :]
            rep_ref[t, part * LANES : (part + 1) * LANES, :] = jnp.broadcast_to(
                row, (LANES, LANES)
            ).T
        return 0

    lax.fori_loop(0, rep_ref.shape[0], step, 0)


def spread_accum(touched, accum):
    touch = touched.shape[1]
    return call(
        spread_kernel,
        2.0,
        8,
        out_shape=like((touch, BLOCK, LANES)),
        in_specs=[HBM, HBM],
        out_specs=VMEM,
        scratch_shapes=[
            pltpu.SMEM((1, touch), jnp.int32),
            pltpu.VMEM(accum.shape, accum.dtype),
            pltpu.SemaphoreType.DMA((2,)),
        ],
    )(touched, accum)


def update_kernel(
    limit, touched_hbm, square_ref, sums_ref, table_ref, accum_rep_ref, mean_rep_ref,
    gathered_ref, accum_hbm, table_in, out_hbm, new_accum_hbm,
    fresh, turned, accum, listed, sems,
):
    fetch = pltpu.make_async_copy(touched_hbm, listed, sems.at[0])
    fetch_accum = pltpu.make_async_copy(accum_hbm, accum, sems.at[1])
    fetch.start()
    fetch_accum.start()
    touch = fresh.shape[0]
    square = jnp.sum(square_ref[...], axis=0)
    square = jnp.sum(jnp.sum(square, axis=1, keepdims=True), axis=0, keepdims=True)
    turned[...] = gathered_ref[...].T
    factor = limit / jnp.maximum(jnp.sqrt(square), limit)
    factor_sq = factor * factor
    rate = LEARN_RATE * factor
    fetch.wait()

    def step(t, _):
        b = listed[0, t]
        root = lax.rsqrt(accum_rep_ref[t] + factor_sq * mean_rep_ref[t])
        fresh[t] = table_ref[b] * (1.0 - DECAY_RATE) - (rate * sums_ref[t]) * root
        pltpu.make_async_copy(fresh.at[t], out_hbm.at[b], sems.at[2]).start()
        return 0

    fetch_accum.wait()
    for t in range(touch):
        for part in range(PARTS):
            at = pl.ds(listed[0, t] * PARTS + part, 1)
            j = t * PARTS + part
            accum[at, :] = accum[at, :] + factor_sq * turned[j : j + 1, :]
    put = pltpu.make_async_copy(accum, new_accum_hbm, sems.at[3])
    put.start()
    lax.fori_loop(0, touch, step, 0)
    put.wait()
    pltpu.make_async_copy(fresh, fresh, sems.at[2]).wait()


def update(limit, touched, square, sums, table, accum_rep, mean_rep, gathered, accum, table_out):
    return call(
        functools.partial(update_kernel, limit),
        2.5,
        8,
        out_shape=(like(table.shape, table.dtype), like(accum.shape, accum.dtype)),
        in_specs=[HBM] + [VMEM] * 6 + [HBM] * 2,
        out_specs=(HBM, HBM),
        scratch_shapes=[
            pltpu.VMEM(sums.shape, table.dtype),
            pltpu.VMEM((LANES, LANES), jnp.float32),
            pltpu.VMEM(accum.shape, accum.dtype),
            pltpu.SMEM(touched.shape, jnp.int32),
            pltpu.SemaphoreType.DMA((4,)),
        ],
        input_output_aliases={8: 0},
    )(touched, square, sums, table, accum_rep, mean_rep, gathered, accum, table_out)


def exchange(x):
    return lax.all_to_all(x, "shard", 0, 0, tiled=True)


def step(row_ids, grad_rows, touched, block_home, embed_table, row_accum):
    slots, width = grad_rows.shape[3:]
    blocks_here = embed_table.shape[0] // BLOCK
    touch = touched.shape[1]
    shards = lax.axis_size("shard")
    reps = lax.axis_size("rep")
    limit = CLIP_RMS * math.sqrt(shards * touch * BLOCK * width)
    ids, grads = row_ids[0, 0], grad_rows[0, 0]
    table = embed_table.reshape(blocks_here, BLOCK, width)
    accum = row_accum.reshape(-1, LANES)
    home = jnp.pad(block_home, (0, -block_home.shape[0] % LANES)).reshape(-1, LANES)
    direct = EARLY if shards > EARLY and EARLY * slots >= TILE else 0

    def swap(x, r=0):
        pairs = [
            (rep * shards + i, (rep + 1) % reps * shards + (i ^ r))
            for rep in range(reps)
            for i in range(shards)
        ]
        return lax.ppermute(x, ("rep", "shard"), pairs)

    data, *early = pack(ids, home, grads, blocks_here, direct)
    data = exchange(data)
    early = [swap(each, r) for r, each in enumerate(early)]
    table_out, slot = keep_untouched(touched, table)
    if direct:
        far_a, far_b = pick_far(data, direct)
    else:
        far_a, far_b = data[: shards // 2], data[shards // 2 :]
    far_a = swap(far_a)
    far_b = swap(far_b)
    (sums,) = sums_of(slot, [data], slots, touch)
    if direct:
        (sums,) = sums_of(slot, early, slots, touch, sums)
    accum_rep = spread_accum(touched, accum)
    (sums,) = sums_of(slot, [far_a], slots, touch, sums)
    sums, mean_rep, gathered, square = sums_of(slot, [far_b], slots, touch, sums, shards)
    square = exchange(square)
    table_out, accum_out = update(
        limit, touched, square, sums, table, accum_rep, mean_rep, gathered, accum, table_out
    )
    return table_out.reshape(-1, width), accum_out.reshape(-1)


def solution(mesh):
    shards = mesh.shape["shard"]
    assert mesh.shape["rep"] == 2 and shards & (shards - 1) == 0
    in_specs = (
        P("rep", "shard", None, None),
        P("rep", "shard", None, None, None),
        P("shard", None),
        P(),
        P("shard", None),
        P("shard"),
    )
    out_specs = (P("shard", None), P("shard"))
    return jax.shard_map(step, mesh=mesh, in_specs=in_specs, out_specs=out_specs, check_vma=False)
```

time: 59.5 us -> 79.2 us (1.33)
  waiting for transfers between devices: 2.67 us -> 11.8 us
  local copies, waits for them, and re-layouts: 0.75 us -> 9.68 us
  starting transfers between devices: 8.46 us -> 9.46 us
    unnamed x10 -> x16, local copies, waits for them, and re-layouts: 0.71 us -> 9.68 us
    ppermute x8 -> x6, waiting for transfers between devices: 2.67 us -> 9.06 us  [swap(): return lax.ppermute(x, ('rep', 'shard'), pairs)]
    all_to_all x0 -> x1, starting transfers between devices: none -> 4.95 us  [exchange(): return lax.all_to_all(x, 'shard', 0, 0, tiled=True)]
    ppermute x8 -> x6, starting transfers between devices: 8.46 us -> 4.51 us  [swap(): return lax.ppermute(x, ('rep', 'shard'), pairs)]
    all_to_all x0 -> x1, waiting for transfers between devices: none -> 2.76 us  [exchange(): return lax.all_to_all(x, 'shard', 0, 0, tiled=True)]
  transfers between devices with their start and end apart: 8 -> 7, of which waited for: 3 -> 2; matrix products, arithmetic and copies ran while one was open for 0% -> 0% of each run, Pallas kernels for 27% -> 19%
where the time goes in v3:
time: 79.2 us; the launch traced here: 78.7 us
  blocking collectives  24.1 us (30%)
  Pallas kernels  22.9 us (29%)
  waiting for transfers between devices  11.8 us (15%)
  local copies, waits for them, and re-layouts  9.68 us (12%)
  starting transfers between devices  9.46 us (12%)
    all_to_all x1, blocking collectives, exchange(): return lax.all_to_all(x, 'shard', 0, 0, tiled=True)  24.1 us
    pallas_call x4, Pallas kernels, sums_of(): call(functools.partial(add_rows, slots, count, fresh, last), slabs * slot...  10.8 us
    unnamed x16, local copies, waits for them, and re-layouts  9.68 us
    ppermute x6, waiting for transfers between devices, swap(): return lax.ppermute(x, ('rep', 'shard'), pairs)  9.06 us
    all_to_all x1, starting transfers between devices, exchange(): return lax.all_to_all(x, 'shard', 0, 0, tiled=True)  4.95 us
    pallas_call x1, Pallas kernels, keep_untouched(): call(keep_kernel, 4.0, 60, out_shape=(like(table.shape, table.dtype), lik...  4.71 us
    ppermute x6, starting transfers between devices, swap(): return lax.ppermute(x, ('rep', 'shard'), pairs)  4.51 us
    all_to_all x1, waiting for transfers between devices, exchange(): return lax.all_to_all(x, 'shard', 0, 0, tiled=True)  2.76 us
  transfers between devices with their start and end apart: 7, of which 2 were waited for; matrix products, arithmetic and copies ran while one was open for 0% of the time, Pallas kernels for 19%

profile of v3, /device:TPU:0, one launch (start us, length us, event | category | flops | bytes accessed | tf_op | source)
XLA Modules:
  0.0 78.7 jit_solution(6642913907976897795)
XLA Ops:
  0.6 2.0 %shard_map.78 = (bf16[16,136,128]{2,1,0:T(8,128)(2,1)}, bf16[1,136,128]{2,1,0:T(8,128)(2,1)}, bf16[1,136,128]{2,1,0:T(8,128)(2,1)}, bf16[1,136,128]{2,1,0:T(8,128)(2,1)}, bf16[1,136,128]{2,1,0:T(8,128)(2,1)}) custom-call(s32[16,128]{1,0:T(8,128)} %bitcast.13, s32[5,128]{1,0:T(8,128)} %bitcast.14, bf16[16,128,128]{2,1,0:T(8,128)(2,1)} %bitcast.12), custom_call_target="tpu_custom_call" | custom-call | flops 4000000 | bytes 1048576 | tf_op jit(solution)/shard_map/pallas_call | solution.py:93
  2.6 24.1 %all_to_all.10.data_ref.refs_0_ = bf16[16,136,128]{2,1,0:T(8,128)(2,1)S(1)} all-to-all(bf16[16,136,128]{2,1,0:T(8,128)(2,1)} %get-tuple-element.18), channel_id=1, replica_groups=mesh['rep'=2,'shard'=16] {'shard'}, dimensions={0} | all-to-all | bytes 1114112 | tf_op jit(solution)/shard_map/all_to_all | solution.py:394
  26.7 0.7 shard_map.79
  27.4 1.5 %collective-permute-start.1 = (bf16[8,136,128]{2,1,0:T(8,128)(2,1)S(1)}, bf16[8,136,128]{2,1,0:T(8,128)(2,1)S(1)}, u32[]{:S(2)}, u32[]{:S(2)}) collective-permute-start(bf16[8,136,128]{2,1,0:T(8,128)(2,1)S(1)} %get-tuple-element.20), channel_id=1, source_target_pairs={{0,16},{1,17},{2,18},{3,19},{4,20},{5,21},{6,22},{7,23},{8,24},{9,... | collective-permute-start | bytes 835592 | tf_op jit(solution)/shard_map/ppermute | solution.py:416
  28.9 0.5 collective-permute-start
  29.4 1.5 %collective-permute-start.2 = (bf16[1,136,128]{2,1,0:T(8,128)(2,1)}, bf16[1,136,128]{2,1,0:T(8,128)(2,1)S(1)}, u32[]{:S(2)}, u32[]{:S(2)}) collective-permute-start(bf16[1,136,128]{2,1,0:T(8,128)(2,1)} %get-tuple-element.21), channel_id=1, source_target_pairs={{0,16},{1,17},{2,18},{3,19},{4,20},{5,21},{6,22},{7,23},{8,24},{9,... | collective-permute-start | bytes 104456 | tf_op jit(solution)/shard_map/ppermute | solution.py:416
  30.9 0.0 collective-permute-start.3
  30.9 0.9 %collective-permute-start.4 = (bf16[1,136,128]{2,1,0:T(8,128)(2,1)}, bf16[1,136,128]{2,1,0:T(8,128)(2,1)S(1)}, u32[]{:S(2)}, u32[]{:S(2)}) collective-permute-start(bf16[1,136,128]{2,1,0:T(8,128)(2,1)} %get-tuple-element.23), channel_id=1, source_target_pairs={{0,18},{1,19},{2,16},{3,17},{4,22},{5,23},{6,20},{7,21},{8,26},{9,... | collective-permute-start | bytes 104456 | tf_op jit(solution)/shard_map/ppermute | solution.py:416
  31.8 9.1 %collective-permute-done.2.refs_0_ = bf16[1,136,128]{2,1,0:T(8,128)(2,1)S(1)} collective-permute-done((bf16[1,136,128]{2,1,0:T(8,128)(2,1)}, bf16[1,136,128]{2,1,0:T(8,128)(2,1)S(1)}, u32[]{:S(2)}, u32[]{:S(2)}) %collective-permute-start.2) | collective-permute-done | bytes 34848 | tf_op jit(solution)/shard_map/ppermute | solution.py:416
  40.9 0.0 collective-permute-start.5
  40.9 4.7 %shard_map.77 = (f32[40,256,128]{2,1,0:T(8,128)}, s32[8,128]{1,0:T(8,128)}) custom-call(s32[1,20]{1,0:T(1,128)} %touched_hbm.5, f32[40,256,128]{2,1,0:T(8,128)} %bitcast.7), custom_call_target="tpu_custom_call" | custom-call | flops 16000000 | bytes 1048576 | tf_op jit(solution)/shard_map/pallas_call | solution.py:185
  45.6 0.0 copy-start.6
  45.7 0.7 copy-done.6
  46.3 3.9 %shard_map.80.refs_4_ = f32[20,256,128]{2,1,0:T(8,128)S(1)} custom-call(s32[8,128]{1,0:T(8,128)S(1)} %copy-done.6, bf16[16,136,128]{2,1,0:T(8,128)(2,1)S(1)} %all_to_all.10.data_ref.refs_0_), custom_call_target="tpu_custom_call" | custom-call | flops 16000000 | bytes 1048576 | tf_op jit(solution)/shard_map/pallas_call | solution.py:288
  50.2 0.0 collective-permute-done.3.refs_1_
  50.2 0.0 collective-permute-done.4.refs_2_
  50.2 0.0 collective-permute-done.5.refs_3_
  50.2 1.7 %shard_map.81.refs_1_ = f32[20,256,128]{2,1,0:T(8,128)S(1)} custom-call(s32[8,128]{1,0:T(8,128)S(1)} %copy-done.6, bf16[1,136,128]{2,1,0:T(8,128)(2,1)S(1)} %collective-permute-done.2.refs_0_, bf16[1,136,128]{2,1,0:T(8,128)(2,1)S(1)} %collective-permute-done.3.refs_1_, ...), custom_call_target="tpu_custom_call", output_to_operand_aliasing={{}: (5, {})} | custom-call | flops 4000000 | bytes 1048576 | tf_op jit(solution)/shard_map/pallas_call | solution.py:288
  51.9 0.0 collective-permute-done.1.refs_0_
  52.0 2.5 %shard_map.82.refs_1_ = f32[20,256,128]{2,1,0:T(8,128)S(1)} custom-call(s32[8,128]{1,0:T(8,128)S(1)} %copy-done.6, bf16[8,136,128]{2,1,0:T(8,128)(2,1)S(1)} %collective-permute-done.1.refs_0_, f32[20,256,128]{2,1,0:T(8,128)S(1)} %shard_map.81.refs_1_), custom_call_target="tpu_custom_call", output_to_operand_aliasing={{}: (2, {})} | custom-call | flops 8000000 | bytes 1048576 | tf_op jit(solution)/shard_map/pallas_call | solution.py:288
  54.4 0.0 copy-start.5
  54.4 0.0 copy-start.7
  54.4 0.0 collective-permute-done.refs_0_
  54.4 2.8 %shard_map.83 = (f32[20,256,128]{2,1,0:T(8,128)S(1)}, f32[20,256,128]{2,1,0:T(8,128)S(1)}, f32[128,128]{1,0:T(8,128)S(1)}, f32[16,8,128]{2,1,0:T(8,128)}) custom-call(s32[8,128]{1,0:T(8,128)S(1)} %copy-done.6, bf16[4,136,128]{2,1,0:T(8,128)(2,1)S(1)} %collective-permute-done.refs_0_, ...), custom_call_target="tpu_custom_call", output_to_operand_aliasing={{0}: (2, {})} | custom-call | flops 4000000 | bytes 1048576 | tf_op jit(solution)/shard_map/pallas_call | solution.py:288
  57.2 0.0 copy-start.3
  57.2 1.5 %copy-done.3 = f32[20,256,128]{2,1,0:T(8,128)} copy-done((f32[20,256,128]{2,1,0:T(8,128)}, f32[20,256,128]{2,1,0:T(8,128)S(1)}, u32[]{:S(2)}) %copy-start.3) | copy-done | bytes 2621464
  58.7 5.0 %all-to-all-start.1 = ((f32[16,8,128]{2,1,0:T(8,128)}), f32[16,8,128]{2,1,0:T(8,128)S(1)}, u32[]{:S(2)}, u32[]{:S(2)}) async-start(f32[16,8,128]{2,1,0:T(8,128)} %get-tuple-element.25), calls=%async_computation.1 | async-start | bytes 131072 | tf_op jit(solution)/shard_map/all_to_all | solution.py:394
  63.7 0.0 copy-done.5
  63.7 0.0 copy-done.7
  63.7 2.6 %shard_map.84.accum_rep_ref = f32[20,256,128]{2,1,0:T(8,128)S(1)} custom-call(s32[1,20]{1,0:T(1,128)S(1)} %copy-done.7, f32[80,128]{1,0:T(8,128)S(1)} %bitcast.9), custom_call_target="tpu_custom_call" | custom-call | flops 8000000 | bytes 1048576 | tf_op jit(solution)/shard_map/pallas_call | solution.py:321
  66.3 0.0 copy-start.1
  66.3 1.5 %copy-done.1 = f32[20,256,128]{2,1,0:T(8,128)} copy-done((f32[20,256,128]{2,1,0:T(8,128)}, f32[20,256,128]{2,1,0:T(8,128)S(1)}, u32[]{:S(2)}) %copy-start.1) | copy-done | bytes 2621464
  67.8 2.8 %all-to-all-done.1.square_ref = f32[16,8,128]{2,1,0:T(8,128)S(1)} async-done(((f32[16,8,128]{2,1,0:T(8,128)}), f32[16,8,128]{2,1,0:T(8,128)S(1)}, u32[]{:S(2)}, u32[]{:S(2)}) %all-to-all-start.1) | async-done | bytes 65568 | tf_op jit(solution)/shard_map/all_to_all | solution.py:394
  70.6 0.0 copy-start
  70.6 2.5 %copy-done = f32[10240,128]{1,0:T(8,128)S(1)} copy-done((f32[10240,128]{1,0:T(8,128)S(1)}, f32[10240,128]{1,0:T(8,128)}, u32[]{:S(2)}) %copy-start) | copy-done | bytes 5242904
  73.1 0.0 copy-start.2
  73.1 1.7 %copy-done.2 = f32[20,256,128]{2,1,0:T(8,128)S(1)} copy-done((f32[20,256,128]{2,1,0:T(8,128)S(1)}, f32[20,256,128]{2,1,0:T(8,128)}, u32[]{:S(2)}) %copy-start.2) | copy-done | bytes 2621464
  74.8 0.0 copy-start.4
  74.8 1.7 %copy-done.4 = f32[20,256,128]{2,1,0:T(8,128)S(1)} copy-done((f32[20,256,128]{2,1,0:T(8,128)S(1)}, f32[20,256,128]{2,1,0:T(8,128)}, u32[]{:S(2)}) %copy-start.4) | copy-done | bytes 2621464
  76.6 2.2 %shard_map.85 = (f32[40,256,128]{2,1,0:T(8,128)}, f32[80,128]{1,0:T(8,128)}) custom-call(s32[1,20]{1,0:T(1,128)S(1)} %copy-done.7, f32[16,8,128]{2,1,0:T(8,128)S(1)} %all-to-all-done.1.square_ref, f32[20,256,128]{2,1,0:T(8,128)S(1)} %get-tuple-element.26.sums_ref, f32[40,256,128]{2,1,0:T(8,128)S(1)} %bitcast.8, ...), custom_call_target="tpu_custom_call", output_to_operand_aliasing={{0}: (8, {})} | custom-call | flops 10000000 | bytes 1048576 | tf_op jit(solution)/shard_map/pallas_call | solution.py:375
Async XLA Ops:
  27.4 24.6 %collective-permute-start.1 = (bf16[8,136,128]{2,1,0:T(8,128)(2,1)S(1)}, bf16[8,136,128]{2,1,0:T(8,128)(2,1)S(1)}, u32[]{:S(2)}, u32[]{:S(2)}) collective-permute-start(bf16[8,136,128]{2,1,0:T(8,128)(2,1)S(1)} %get-tuple-element.20), channel_id=1, source_target_pairs={{0,16},{1,17},{2,18},{3,19},{4,20},{5,21},{6,22},{7,23},{8,24},{9,... | collective-permute-start | bytes 835592 | tf_op jit(solution)/shard_map/ppermute | solution.py:416
  28.9 25.6 %collective-permute-start = (bf16[4,136,128]{2,1,0:T(8,128)(2,1)}, bf16[4,136,128]{2,1,0:T(8,128)(2,1)S(1)}, u32[]{:S(2)}, u32[]{:S(2)}) collective-permute-start(bf16[4,136,128]{2,1,0:T(8,128)(2,1)} %get-tuple-element.19), channel_id=1, source_target_pairs={{0,16},{1,17},{2,18},{3,19},{4,20},{5,21},{6,22},{7,23},{8,24},{9,... | collective-permute-start | bytes 417800 | tf_op jit(solution)/shard_map/ppermute | solution.py:416
  29.4 11.5 %collective-permute-start.2 = (bf16[1,136,128]{2,1,0:T(8,128)(2,1)}, bf16[1,136,128]{2,1,0:T(8,128)(2,1)S(1)}, u32[]{:S(2)}, u32[]{:S(2)}) collective-permute-start(bf16[1,136,128]{2,1,0:T(8,128)(2,1)} %get-tuple-element.21), channel_id=1, source_target_pairs={{0,16},{1,17},{2,18},{3,19},{4,20},{5,21},{6,22},{7,23},{8,24},{9,... | collective-permute-start | bytes 104456 | tf_op jit(solution)/shard_map/ppermute | solution.py:416
  30.9 19.3 %collective-permute-start.3 = (bf16[1,136,128]{2,1,0:T(8,128)(2,1)}, bf16[1,136,128]{2,1,0:T(8,128)(2,1)S(1)}, u32[]{:S(2)}, u32[]{:S(2)}) collective-permute-start(bf16[1,136,128]{2,1,0:T(8,128)(2,1)} %get-tuple-element.22), channel_id=1, source_target_pairs={{0,17},{1,16},{2,19},{3,18},{4,21},{5,20},{6,23},{7,22},{8,25},{9,... | collective-permute-start | bytes 104456 | tf_op jit(solution)/shard_map/ppermute | solution.py:416
  30.9 19.3 %collective-permute-start.4 = (bf16[1,136,128]{2,1,0:T(8,128)(2,1)}, bf16[1,136,128]{2,1,0:T(8,128)(2,1)S(1)}, u32[]{:S(2)}, u32[]{:S(2)}) collective-permute-start(bf16[1,136,128]{2,1,0:T(8,128)(2,1)} %get-tuple-element.23), channel_id=1, source_target_pairs={{0,18},{1,19},{2,16},{3,17},{4,22},{5,23},{6,20},{7,21},{8,26},{9,... | collective-permute-start | bytes 104456 | tf_op jit(solution)/shard_map/ppermute | solution.py:416
  40.9 9.3 %collective-permute-start.5 = (bf16[1,136,128]{2,1,0:T(8,128)(2,1)}, bf16[1,136,128]{2,1,0:T(8,128)(2,1)S(1)}, u32[]{:S(2)}, u32[]{:S(2)}) collective-permute-start(bf16[1,136,128]{2,1,0:T(8,128)(2,1)} %get-tuple-element.24), channel_id=1, source_target_pairs={{0,19},{1,18},{2,17},{3,16},{4,23},{5,22},{6,21},{7,20},{8,27},{9,... | collective-permute-start | bytes 104456 | tf_op jit(solution)/shard_map/ppermute | solution.py:416
  45.6 0.7 copy-start.6
  54.4 9.3 %copy-start.5 = (f32[10240]{0:T(1024)S(1)}, f32[10240]{0:T(1024)}, u32[]{:S(2)}) copy-start(f32[10240]{0:T(1024)} %param.11) | copy-start | bytes 122884
  54.4 9.3 %copy-start.7 = (s32[1,20]{1,0:T(1,128)S(1)}, s32[1,20]{1,0:T(1,128)}, u32[]{:S(2)}) copy-start(s32[1,20]{1,0:T(1,128)} %touched_hbm.5) | copy-start | bytes 244
  57.2 1.5 %copy-start.3 = (f32[20,256,128]{2,1,0:T(8,128)}, f32[20,256,128]{2,1,0:T(8,128)S(1)}, u32[]{:S(2)}) copy-start(f32[20,256,128]{2,1,0:T(8,128)S(1)} %get-tuple-element.27.mean_rep_ref) | copy-start | bytes 7864324
  58.7 11.9 %all-to-all-start.1 = ((f32[16,8,128]{2,1,0:T(8,128)}), f32[16,8,128]{2,1,0:T(8,128)S(1)}, u32[]{:S(2)}, u32[]{:S(2)}) async-start(f32[16,8,128]{2,1,0:T(8,128)} %get-tuple-element.25), calls=%async_computation.1 | async-start | bytes 131072 | tf_op jit(solution)/shard_map/all_to_all | solution.py:394
  66.3 1.5 %copy-start.1 = (f32[20,256,128]{2,1,0:T(8,128)}, f32[20,256,128]{2,1,0:T(8,128)S(1)}, u32[]{:S(2)}) copy-start(f32[20,256,128]{2,1,0:T(8,128)S(1)} %shard_map.84.accum_rep_ref) | copy-start | bytes 7864324
  70.6 2.5 %copy-start = (f32[10240,128]{1,0:T(8,128)S(1)}, f32[10240,128]{1,0:T(8,128)}, u32[]{:S(2)}) copy-start(f32[10240,128]{1,0:T(8,128)} %param.10) | copy-start | bytes 15728644
  73.1 1.7 %copy-start.2 = (f32[20,256,128]{2,1,0:T(8,128)S(1)}, f32[20,256,128]{2,1,0:T(8,128)}, u32[]{:S(2)}) copy-start(f32[20,256,128]{2,1,0:T(8,128)} %copy-done.1) | copy-start | bytes 7864324
  74.8 1.7 %copy-start.4 = (f32[20,256,128]{2,1,0:T(8,128)S(1)}, f32[20,256,128]{2,1,0:T(8,128)}, u32[]{:S(2)}) copy-start(f32[20,256,128]{2,1,0:T(8,128)} %copy-done.3) | copy-start | bytes 7864324

commit v4 on v3

--- a/solution.py
+++ b/solution.py
@@ -24,6 +24,7 @@
 HBM = pl.BlockSpec(memory_space=pltpu.HBM)
 
 EARLY = 4
+CHUNKS = 4
 
 
 def call(kernel, us, mib, **kwargs):
@@ -41,23 +42,23 @@
     return jax.ShapeDtypeStruct(shape, dtype)
 
 
-def pack_kernel(slots, blocks_here, ids_hbm, home_hbm, grads_hbm, out_ref, *rest):
-    early, (ids_ref, home_ref, digits_ref, sems) = rest[:-4], rest[-4:]
+def pack_kernel(slots, blocks_here, ids_hbm, home_hbm, grads_hbm, out_hbm, *rest):
+    early, (ids_ref, home_ref, buffer, sems, load_sems) = rest[:-5], rest[-5:]
+    groups = ids_ref.shape[0]
     fetch = pltpu.make_async_copy(ids_hbm, ids_ref, sems.at[0])
     fetch_home = pltpu.make_async_copy(home_hbm, home_ref, sems.at[1])
-    copy = pltpu.make_async_copy(grads_hbm, out_ref.at[:, pl.ds(0, slots), :], sems.at[2])
     fetch.start()
     fetch_home.start()
-    copy.start()
-    me = lax.axis_index("shard")
-    copies = [
-        pltpu.make_async_copy(
-            grads_hbm.at[me ^ r], early[r].at[0, pl.ds(0, slots), :], sems.at[3 + r]
+    chunk = groups // CHUNKS
+    loads = []
+    for c in range(CHUNKS):
+        at = pl.ds(c * chunk, chunk)
+        loads.append(
+            pltpu.make_async_copy(
+                grads_hbm.at[at], buffer.at[at, pl.ds(0, slots), :], load_sems.at[c]
+            )
         )
-        for r in range(len(early))
-    ]
-    for each in copies:
-        each.start()
+        loads[c].start()
     row = lax.broadcasted_iota(jnp.int32, (META, LANES), 0)
     fetch.wait()
     fetch_home.wait()
@@ -71,38 +72,45 @@
     owner = lax.broadcasted_iota(jnp.int32, ids.shape, 0)
     local = jnp.where(ids >= 0, home - owner * blocks_here, LANES - 1).astype(jnp.float32)
     within = (ids & (BLOCK - 1)).astype(jnp.float32)
-    for group in range(ids.shape[0]):
+    for group in range(groups):
         here = jnp.broadcast_to(local[group : group + 1, :], row.shape)
         there = jnp.broadcast_to(within[group : group + 1, :], row.shape)
         digits = jnp.where(row == 0, here, there)
-        out_ref[group, slots : slots + META, :] = digits.astype(jnp.bfloat16)
-        digits_ref[group] = digits
+        buffer[group, slots : slots + META, :] = digits.astype(jnp.bfloat16)
+    stores = []
+    for c in range(CHUNKS):
+        loads[c].wait()
+        at = pl.ds(c * chunk, chunk)
+        stores.append(pltpu.make_async_copy(buffer.at[at], out_hbm.at[at], load_sems.at[c]))
+        stores[c].start()
+    me = lax.axis_index("shard")
     for r, ref in enumerate(early):
-        ref[0, slots : slots + META, :] = digits_ref[me ^ r].astype(jnp.bfloat16)
-    for each in copies:
+        stores.append(pltpu.make_async_copy(buffer.at[me ^ r], ref.at[0], sems.at[2 + r]))
+        stores[-1].start()
+    for each in stores:
         each.wait()
-    copy.wait()
 
 
 def pack(ids, home, grads, blocks_here, early):
     groups, slots, width = grads.shape
     pad = LANES - slots
     ids = jnp.pad(ids, ((0, 0), (0, pad)), constant_values=-1) if pad else ids
-    assert blocks_here < LANES
+    assert blocks_here < LANES and groups % CHUNKS == 0
     slab = (slots + META, width)
     return call(
         functools.partial(pack_kernel, slots, blocks_here),
         1.0,
-        62.9,
+        64,
         out_shape=(like((groups, *slab), grads.dtype),)
         + (like((1, *slab), grads.dtype),) * early,
         in_specs=[HBM] * 3,
-        out_specs=(VMEM,) * (1 + early),
+        out_specs=(HBM,) * (1 + early),
         scratch_shapes=[
             pltpu.VMEM((groups, LANES), jnp.int32),
             pltpu.VMEM(home.shape, jnp.int32),
-            pltpu.VMEM((groups, META, LANES), jnp.float32),
-            pltpu.SemaphoreType.DMA((3 + early,)),
+            pltpu.VMEM((groups, *slab), grads.dtype),
+            pltpu.SemaphoreType.DMA((2 + early,)),
+            pltpu.SemaphoreType.DMA((CHUNKS,)),
         ],
     )(ids, home, grads)
 
@@ -136,7 +144,7 @@
     )(data)
 
 
-def keep_kernel(touched_hbm, table_hbm, out_hbm, slot_ref, listed, bounce, other, sems):
+def keep_kernel(touched_hbm, table_hbm, out_hbm, listed, bounce, other, sems):
     blocks, touch = table_hbm.shape[0], touched_hbm.shape[1]
     fetch = pltpu.make_async_copy(touched_hbm, listed, sems.at[0])
     fetch.start()
@@ -148,14 +156,11 @@
     lax.fori_loop(0, blocks, clear, 0)
     fetch.wait()
 
-    lane = lax.broadcasted_iota(jnp.int32, slot_ref.shape, 1)
-
-    def mark(t, slot):
-        b = listed[0, t]
-        other[b] = 1
-        return jnp.where(lane == b, t, slot)
-
-    slot_ref[...] = lax.fori_loop(0, touch, mark, jnp.full(slot_ref.shape, -1, jnp.int32))
+    def mark(t, _):
+        other[listed[0, t]] = 1
+        return 0
+
+    lax.fori_loop(0, touch, mark, 0)
 
     def pull(b, count):
         free = other[b] == 0
@@ -186,9 +191,9 @@
         keep_kernel,
         4.0,
         60,
-        out_shape=(like(table.shape, table.dtype), like((8, LANES), jnp.int32)),
+        out_shape=like(table.shape, table.dtype),
         in_specs=[HBM, HBM],
-        out_specs=(HBM, VMEM),
+        out_specs=HBM,
         scratch_shapes=[
             pltpu.SMEM((1, touch), jnp.int32),
             pltpu.VMEM((blocks - touch, BLOCK, width), table.dtype),
@@ -241,10 +246,11 @@
         flat = [jnp.where(key >= 0, (key >> 8) * LANES + (key & (LANES - 1)), -1) for key in pair]
         key_rows.append(jnp.concatenate(flat, axis=1))
     row = lax.broadcasted_iota(jnp.int32, (many * LANES, TILE), 0)
-    lane = lax.broadcasted_iota(jnp.int32, (LANES, LANES), 1)
     if last:
-        mean_rep_ref, gathered_ref, square_ref = refs[2:5]
-        gathered_ref[...] = jnp.zeros_like(gathered_ref)
+        own_lane = lax.broadcasted_iota(jnp.int32, (LANES, LANES), 0) == (
+            lax.broadcasted_iota(jnp.int32, (LANES, LANES), 1)
+        )
+        mean_rep_ref, flat_ref, square_ref = refs[2:5]
 
     def step(u, carry):
         total = None
@@ -264,14 +270,13 @@
                     mean = jnp.sum(piece * piece, axis=1, keepdims=True) * (1.0 / width)
                     mean = jnp.broadcast_to(mean, (LANES, LANES))
                     mean_rep_ref[t, at, :] = mean
-                    gathered_ref[...] = jnp.where(
-                        lane == t * PARTS + p, mean, gathered_ref[...]
-                    )
+                    line = jnp.sum(jnp.where(own_lane, mean, 0.0), axis=0, keepdims=True)
+                    flat_ref[pl.ds(t * PARTS + p, 1), :] = line
         return carry
 
     lax.fori_loop(0, touch // many, step, 0)
     if last:
-        square = jnp.sum(gathered_ref[...].reshape(-1, 8, LANES), axis=0) * width
+        square = jnp.sum(flat_ref[...].reshape(-1, 8, LANES), axis=0) * width
         for i in range(square_ref.shape[0]):
             square_ref[i] = square
 
@@ -281,10 +286,14 @@
     count = len(data)
     slabs = sum(each.shape[0] for each in data)
     fresh, last = sums is None, shards > 0
-    assert slabs * slots % TILE == 0 and touch * PARTS <= LANES
+    assert slabs * slots % TILE == 0 and touch * PARTS % 8 == 0
     outs = (like((touch, BLOCK, width)),)
     if last:
-        outs += (like((touch, BLOCK, LANES)), like((LANES, LANES)), like((shards, 8, LANES)))
+        outs += (
+            like((touch, BLOCK, LANES)),
+            like((touch * PARTS, LANES)),
+            like((shards, 8, LANES)),
+        )
     return call(
         functools.partial(add_rows, slots, count, fresh, last),
         slabs * slots / 512,
@@ -297,23 +306,26 @@
     )(slot, *data, *([] if fresh else [sums]))
 
 
-def spread_kernel(touched_hbm, accum_hbm, rep_ref, listed, accum, sems):
+def spread_kernel(touched_hbm, accum_hbm, rep_ref, slot_ref, listed, accum, sems):
     a = pltpu.make_async_copy(touched_hbm, listed, sems.at[0])
     b = pltpu.make_async_copy(accum_hbm, accum, sems.at[1])
     a.start()
     b.start()
     a.wait()
     b.wait()
-
-    def step(t, _):
+    lane = lax.broadcasted_iota(jnp.int32, slot_ref.shape, 1)
+
+    def step(t, slot):
+        block = listed[0, t]
         for part in range(PARTS):
-            row = accum[pl.ds(listed[0, t] * PARTS + part, 1), :]
+            row = accum[pl.ds(block * PARTS + part, 1), :]
             rep_ref[t, part * LANES : (part + 1) * LANES, :] = jnp.broadcast_to(
                 row, (LANES, LANES)
             ).T
-        return 0
-
-    lax.fori_loop(0, rep_ref.shape[0], step, 0)
+        return jnp.where(lane == block, t, slot)
+
+    start = jnp.full(slot_ref.shape, -1, jnp.int32)
+    slot_ref[...] = lax.fori_loop(0, rep_ref.shape[0], step, start)
 
 
 def spread_accum(touched, accum):
@@ -322,9 +334,9 @@
         spread_kernel,
         2.0,
         8,
-        out_shape=like((touch, BLOCK, LANES)),
+        out_shape=(like((touch, BLOCK, LANES)), like((8, LANES), jnp.int32)),
         in_specs=[HBM, HBM],
-        out_specs=VMEM,
+        out_specs=(VMEM, VMEM),
         scratch_shapes=[
             pltpu.SMEM((1, touch), jnp.int32),
             pltpu.VMEM(accum.shape, accum.dtype),
@@ -335,8 +347,7 @@
 
 def update_kernel(
     limit, touched_hbm, square_ref, sums_ref, table_ref, accum_rep_ref, mean_rep_ref,
-    gathered_ref, accum_hbm, table_in, out_hbm, new_accum_hbm,
-    fresh, turned, accum, listed, sems,
+    flat_ref, accum_hbm, table_in, out_hbm, new_accum_hbm, fresh, accum, listed, sems,
 ):
     fetch = pltpu.make_async_copy(touched_hbm, listed, sems.at[0])
     fetch_accum = pltpu.make_async_copy(accum_hbm, accum, sems.at[1])
@@ -345,7 +356,6 @@
     touch = fresh.shape[0]
     square = jnp.sum(square_ref[...], axis=0)
     square = jnp.sum(jnp.sum(square, axis=1, keepdims=True), axis=0, keepdims=True)
-    turned[...] = gathered_ref[...].T
     factor = limit / jnp.maximum(jnp.sqrt(square), limit)
     factor_sq = factor * factor
     rate = LEARN_RATE * factor
@@ -363,7 +373,7 @@
         for part in range(PARTS):
             at = pl.ds(listed[0, t] * PARTS + part, 1)
             j = t * PARTS + part
-            accum[at, :] = accum[at, :] + factor_sq * turned[j : j + 1, :]
+            accum[at, :] = accum[at, :] + factor_sq * flat_ref[j : j + 1, :]
     put = pltpu.make_async_copy(accum, new_accum_hbm, sems.at[3])
     put.start()
     lax.fori_loop(0, touch, step, 0)
@@ -371,7 +381,7 @@
     pltpu.make_async_copy(fresh, fresh, sems.at[2]).wait()
 
 
-def update(limit, touched, square, sums, table, accum_rep, mean_rep, gathered, accum, table_out):
+def update(limit, touched, square, sums, table, accum_rep, mean_rep, flat, accum, table_out):
     return call(
         functools.partial(update_kernel, limit),
         2.5,
@@ -381,13 +391,12 @@
         out_specs=(HBM, HBM),
         scratch_shapes=[
             pltpu.VMEM(sums.shape, table.dtype),
-            pltpu.VMEM((LANES, LANES), jnp.float32),
             pltpu.VMEM(accum.shape, accum.dtype),
             pltpu.SMEM(touched.shape, jnp.int32),
             pltpu.SemaphoreType.DMA((4,)),
         ],
         input_output_aliases={8: 0},
-    )(touched, square, sums, table, accum_rep, mean_rep, gathered, accum, table_out)
+    )(touched, square, sums, table, accum_rep, mean_rep, flat, accum, table_out)
 
 
 def exchange(x):
@@ -418,22 +427,20 @@
     data, *early = pack(ids, home, grads, blocks_here, direct)
     data = exchange(data)
     early = [swap(each, r) for r, each in enumerate(early)]
-    table_out, slot = keep_untouched(touched, table)
+    table_out = keep_untouched(touched, table)
+    accum_rep, slot = spread_accum(touched, accum)
     if direct:
         far_a, far_b = pick_far(data, direct)
     else:
         far_a, far_b = data[: shards // 2], data[shards // 2 :]
     far_a = swap(far_a)
     far_b = swap(far_b)
-    (sums,) = sums_of(slot, [data], slots, touch)
-    if direct:
-        (sums,) = sums_of(slot, early, slots, touch, sums)
-    accum_rep = spread_accum(touched, accum)
+    (sums,) = sums_of(slot, [data, *early], slots, touch)
     (sums,) = sums_of(slot, [far_a], slots, touch, sums)
-    sums, mean_rep, gathered, square = sums_of(slot, [far_b], slots, touch, sums, shards)
+    sums, mean_rep, flat, square = sums_of(slot, [far_b], slots, touch, sums, shards)
     square = exchange(square)
     table_out, accum_out = update(
-        limit, touched, square, sums, table, accum_rep, mean_rep, gathered, accum, table_out
+        limit, touched, square, sums, table, accum_rep, mean_rep, flat, accum, table_out
     )
     return table_out.reshape(-1, width), accum_out.reshape(-1)
 

time: 79.2 us -> 77.9 us (0.984)
  Pallas kernels: 22.9 us -> 20.8 us
    pallas_call x4 -> x3, Pallas kernels: 10.8 us -> 9.82 us  [sums_of(): call(functools.partial(add_rows, slots, count, fresh, last), slabs * slot...]
    unnamed x16 -> x18, local copies, waits for them, and re-layouts: 9.68 us -> 10.4 us
  transfers between devices with their start and end apart: 7 -> 7, of which waited for: 2 -> 2; matrix products, arithmetic and copies ran while one was open for 0% -> 0% of each run, Pallas kernels for 19% -> 18%
where the time goes in v4:
time: 77.9 us; the launch traced here: 77.3 us
  blocking collectives  24.1 us (31%)
  Pallas kernels  20.8 us (27%)
  waiting for transfers between devices  11.7 us (15%)
  local copies, waits for them, and re-layouts  10.4 us (13%)
  starting transfers between devices  9.54 us (12%)
    all_to_all x1, blocking collectives, exchange(): return lax.all_to_all(x, 'shard', 0, 0, tiled=True)  24.1 us
    unnamed x18, local copies, waits for them, and re-layouts  10.4 us
    pallas_call x3, Pallas kernels, sums_of(): call(functools.partial(add_rows, slots, count, fresh, last), slabs * slot...  9.82 us
    ppermute x6, waiting for transfers between devices, swap(): return lax.ppermute(x, ('rep', 'shard'), pairs)  9.06 us
    all_to_all x1, starting transfers between devices, exchange(): return lax.all_to_all(x, 'shard', 0, 0, tiled=True)  4.97 us
    ppermute x6, starting transfers between devices, swap(): return lax.ppermute(x, ('rep', 'shard'), pairs)  4.57 us
    pallas_call x1, Pallas kernels, keep_untouched(): call(keep_kernel, 4.0, 60, out_shape=like(table.shape, table.dtype), in_s...  4.25 us
    all_to_all x1, waiting for transfers between devices, exchange(): return lax.all_to_all(x, 'shard', 0, 0, tiled=True)  2.61 us
  transfers between devices with their start and end apart: 7, of which 2 were waited for; matrix products, arithmetic and copies ran while one was open for 0% of the time, Pallas kernels for 18%

profile of v4, /device:TPU:0, one launch (start us, length us, event | category | flops | bytes accessed | tf_op | source)
XLA Modules:
  0.0 77.3 jit_solution(9263537213308538492)
XLA Ops:
  0.6 1.9 %shard_map.78 = (bf16[16,136,128]{2,1,0:T(8,128)(2,1)}, bf16[1,136,128]{2,1,0:T(8,128)(2,1)}, bf16[1,136,128]{2,1,0:T(8,128)(2,1)}, bf16[1,136,128]{2,1,0:T(8,128)(2,1)}, bf16[1,136,128]{2,1,0:T(8,128)(2,1)}) custom-call(s32[16,128]{1,0:T(8,128)} %bitcast.13, s32[5,128]{1,0:T(8,128)} %bitcast.14, bf16[16,128,128]{2,1,0:T(8,128)(2,1)} %bitcast.12), custom_call_target="tpu_custom_call" | custom-call | flops 4000000 | bytes 1048576 | tf_op jit(solution)/shard_map/pallas_call | solution.py:100
  2.5 24.1 %all_to_all.10.data_ref.refs_0_ = bf16[16,136,128]{2,1,0:T(8,128)(2,1)S(1)} all-to-all(bf16[16,136,128]{2,1,0:T(8,128)(2,1)} %get-tuple-element.18), channel_id=1, replica_groups=mesh['rep'=2,'shard'=16] {'shard'}, dimensions={0} | all-to-all | bytes 1114112 | tf_op jit(solution)/shard_map/all_to_all | solution.py:403
  26.7 1.6 %collective-permute-start.1 = (bf16[8,136,128]{2,1,0:T(8,128)(2,1)S(1)}, bf16[8,136,128]{2,1,0:T(8,128)(2,1)S(1)}, u32[]{:S(2)}, u32[]{:S(2)}) collective-permute-start(bf16[8,136,128]{2,1,0:T(8,128)(2,1)S(1)} %get-tuple-element.20), channel_id=1, source_target_pairs={{0,16},{1,17},{2,18},{3,19},{4,20},{5,21},{6,22},{7,23},{8,24},{9,... | collective-permute-start | bytes 835592 | tf_op jit(solution)/shard_map/ppermute | solution.py:425
  28.2 0.5 collective-permute-start
  28.7 1.5 %collective-permute-start.2 = (bf16[1,136,128]{2,1,0:T(8,128)(2,1)}, bf16[1,136,128]{2,1,0:T(8,128)(2,1)S(1)}, u32[]{:S(2)}, u32[]{:S(2)}) collective-permute-start(bf16[1,136,128]{2,1,0:T(8,128)(2,1)} %get-tuple-element.21), channel_id=1, source_target_pairs={{0,16},{1,17},{2,18},{3,19},{4,20},{5,21},{6,22},{7,23},{8,24},{9,... | collective-permute-start | bytes 104456 | tf_op jit(solution)/shard_map/ppermute | solution.py:425
  30.3 0.0 collective-permute-start.3
  30.3 0.9 %collective-permute-start.4 = (bf16[1,136,128]{2,1,0:T(8,128)(2,1)}, bf16[1,136,128]{2,1,0:T(8,128)(2,1)S(1)}, u32[]{:S(2)}, u32[]{:S(2)}) collective-permute-start(bf16[1,136,128]{2,1,0:T(8,128)(2,1)} %get-tuple-element.23), channel_id=1, source_target_pairs={{0,18},{1,19},{2,16},{3,17},{4,22},{5,23},{6,20},{7,21},{8,26},{9,... | collective-permute-start | bytes 104456 | tf_op jit(solution)/shard_map/ppermute | solution.py:425
  31.2 9.1 %collective-permute-done.2.refs_1_ = bf16[1,136,128]{2,1,0:T(8,128)(2,1)S(1)} collective-permute-done((bf16[1,136,128]{2,1,0:T(8,128)(2,1)}, bf16[1,136,128]{2,1,0:T(8,128)(2,1)S(1)}, u32[]{:S(2)}, u32[]{:S(2)}) %collective-permute-start.2) | collective-permute-done | bytes 34848 | tf_op jit(solution)/shard_map/ppermute | solution.py:425
  40.2 0.0 collective-permute-start.5
  40.3 0.0 copy-start.5
  40.3 0.8 %copy-done.5 = f32[10240]{0:T(1024)S(1)} copy-done((f32[10240]{0:T(1024)S(1)}, f32[10240]{0:T(1024)}, u32[]{:S(2)}) %copy-start.5) | copy-done | bytes 40984
  41.1 0.0 copy-start.7
  41.1 0.7 copy-done.7
  41.7 2.6 %shard_map.77 = (f32[20,256,128]{2,1,0:T(8,128)S(1)}, s32[8,128]{1,0:T(8,128)S(1)}) custom-call(s32[1,20]{1,0:T(1,128)S(1)} %copy-done.7, f32[80,128]{1,0:T(8,128)S(1)} %bitcast.9), custom_call_target="tpu_custom_call" | custom-call | flops 8000000 | bytes 1048576 | tf_op jit(solution)/shard_map/pallas_call | solution.py:333
  44.3 0.0 copy-start.1
  44.3 1.5 %copy-done.1 = f32[20,256,128]{2,1,0:T(8,128)} copy-done((f32[20,256,128]{2,1,0:T(8,128)}, f32[20,256,128]{2,1,0:T(8,128)S(1)}, u32[]{:S(2)}) %copy-start.1) | copy-done | bytes 2621464
  45.8 0.0 collective-permute-done.3.refs_2_
  45.8 0.0 collective-permute-done.4.refs_3_
  45.8 0.0 collective-permute-done.5.refs_4_
  45.8 4.6 %shard_map.80.refs_1_ = f32[20,256,128]{2,1,0:T(8,128)S(1)} custom-call(s32[8,128]{1,0:T(8,128)S(1)} %get-tuple-element.17.slot_ref, bf16[16,136,128]{2,1,0:T(8,128)(2,1)S(1)} %all_to_all.10.data_ref.refs_0_, bf16[1,136,128]{2,1,0:T(8,128)(2,1)S(1)} %collective-permute-done.2.refs_1_, bf16[1,136,128]{2,1,0:T(8,128)(2,1)S(1)} %collective-permute-done.3.refs_2_, ...), custom_call_target="tpu_custom_call" | custom-call | flops 20000000 | bytes 1048576 | tf_op jit(solution)/shard_map/pallas_call | solution.py:297
  50.4 0.0 collective-permute-done.1.refs_0_
  50.4 2.4 %shard_map.81.refs_1_ = f32[20,256,128]{2,1,0:T(8,128)S(1)} custom-call(s32[8,128]{1,0:T(8,128)S(1)} %get-tuple-element.17.slot_ref, bf16[8,136,128]{2,1,0:T(8,128)(2,1)S(1)} %collective-permute-done.1.refs_0_, f32[20,256,128]{2,1,0:T(8,128)S(1)} %shard_map.80.refs_1_), custom_call_target="tpu_custom_call", output_to_operand_aliasing={{}: (2, {})} | custom-call | flops 8000000 | bytes 1048576 | tf_op jit(solution)/shard_map/pallas_call | solution.py:297
  52.9 0.0 collective-permute-done.refs_0_
  52.9 2.8 %shard_map.82 = (f32[20,256,128]{2,1,0:T(8,128)S(1)}, f32[20,256,128]{2,1,0:T(8,128)S(1)}, f32[40,128]{1,0:T(8,128)S(1)}, f32[16,8,128]{2,1,0:T(8,128)}) custom-call(s32[8,128]{1,0:T(8,128)S(1)} %get-tuple-element.17.slot_ref, bf16[4,136,128]{2,1,0:T(8,128)(2,1)S(1)} %collective-permute-done.refs_0_, ...), custom_call_target="tpu_custom_call", output_to_operand_aliasing={{0}: (2, {})} | custom-call | flops 4000000 | bytes 1048576 | tf_op jit(solution)/shard_map/pallas_call | solution.py:297
  55.7 0.0 copy-start.3
  55.7 1.5 %copy-done.3 = f32[20,256,128]{2,1,0:T(8,128)} copy-done((f32[20,256,128]{2,1,0:T(8,128)}, f32[20,256,128]{2,1,0:T(8,128)S(1)}, u32[]{:S(2)}) %copy-start.3) | copy-done | bytes 2621464
  57.2 5.0 %all-to-all-start.1 = ((f32[16,8,128]{2,1,0:T(8,128)}), f32[16,8,128]{2,1,0:T(8,128)S(1)}, u32[]{:S(2)}, u32[]{:S(2)}) async-start(f32[16,8,128]{2,1,0:T(8,128)} %get-tuple-element.25), calls=%async_computation.1 | async-start | bytes 131072 | tf_op jit(solution)/shard_map/all_to_all | solution.py:403
  62.2 0.0 copy-start.6
  62.2 0.0 copy-start.8
  62.2 4.3 %shard_map.83.table_in = f32[40,256,128]{2,1,0:T(8,128)} custom-call(s32[1,20]{1,0:T(1,128)} %touched_hbm.5, f32[40,256,128]{2,1,0:T(8,128)} %bitcast.7), custom_call_target="tpu_custom_call" | custom-call | flops 16000000 | bytes 1048576 | tf_op jit(solution)/shard_map/pallas_call | solution.py:190
  66.5 2.6 %all-to-all-done.1.square_ref = f32[16,8,128]{2,1,0:T(8,128)S(1)} async-done(((f32[16,8,128]{2,1,0:T(8,128)}), f32[16,8,128]{2,1,0:T(8,128)S(1)}, u32[]{:S(2)}, u32[]{:S(2)}) %all-to-all-start.1) | async-done | bytes 65568 | tf_op jit(solution)/shard_map/all_to_all | solution.py:403
  69.1 0.0 copy-done.6
  69.1 0.0 copy-done.8
  69.1 0.0 copy-start
  69.1 2.5 %copy-done = f32[10240,128]{1,0:T(8,128)S(1)} copy-done((f32[10240,128]{1,0:T(8,128)S(1)}, f32[10240,128]{1,0:T(8,128)}, u32[]{:S(2)}) %copy-start) | copy-done | bytes 5242904
  71.6 0.0 copy-start.2
  71.6 1.7 %copy-done.2 = f32[20,256,128]{2,1,0:T(8,128)S(1)} copy-done((f32[20,256,128]{2,1,0:T(8,128)S(1)}, f32[20,256,128]{2,1,0:T(8,128)}, u32[]{:S(2)}) %copy-start.2) | copy-done | bytes 2621464
  73.3 0.0 copy-start.4
  73.3 1.7 %copy-done.4 = f32[20,256,128]{2,1,0:T(8,128)S(1)} copy-done((f32[20,256,128]{2,1,0:T(8,128)S(1)}, f32[20,256,128]{2,1,0:T(8,128)}, u32[]{:S(2)}) %copy-start.4) | copy-done | bytes 2621464
  75.1 2.2 %shard_map.84 = (f32[40,256,128]{2,1,0:T(8,128)}, f32[80,128]{1,0:T(8,128)}) custom-call(s32[1,20]{1,0:T(1,128)S(1)} %copy-done.8, f32[16,8,128]{2,1,0:T(8,128)S(1)} %all-to-all-done.1.square_ref, f32[20,256,128]{2,1,0:T(8,128)S(1)} %get-tuple-element.26.sums_ref, f32[40,256,128]{2,1,0:T(8,128)S(1)} %bitcast.8, ...), custom_call_target="tpu_custom_call", output_to_operand_aliasing={{0}: (8, {})} | custom-call | flops 10000000 | bytes 1048576 | tf_op jit(solution)/shard_map/pallas_call | solution.py:385
  (1 shorter events, 0.0 us)
Async XLA Ops:
  26.7 23.8 %collective-permute-start.1 = (bf16[8,136,128]{2,1,0:T(8,128)(2,1)S(1)}, bf16[8,136,128]{2,1,0:T(8,128)(2,1)S(1)}, u32[]{:S(2)}, u32[]{:S(2)}) collective-permute-start(bf16[8,136,128]{2,1,0:T(8,128)(2,1)S(1)} %get-tuple-element.20), channel_id=1, source_target_pairs={{0,16},{1,17},{2,18},{3,19},{4,20},{5,21},{6,22},{7,23},{8,24},{9,... | collective-permute-start | bytes 835592 | tf_op jit(solution)/shard_map/ppermute | solution.py:425
  28.2 24.6 %collective-permute-start = (bf16[4,136,128]{2,1,0:T(8,128)(2,1)S(1)}, bf16[4,136,128]{2,1,0:T(8,128)(2,1)S(1)}, u32[]{:S(2)}, u32[]{:S(2)}) collective-permute-start(bf16[4,136,128]{2,1,0:T(8,128)(2,1)S(1)} %get-tuple-element.19), channel_id=1, source_target_pairs={{0,16},{1,17},{2,18},{3,19},{4,20},{5,21},{6,22},{7,23},{8,24},{9,... | collective-permute-start | bytes 417800 | tf_op jit(solution)/shard_map/ppermute | solution.py:425
  28.7 11.5 %collective-permute-start.2 = (bf16[1,136,128]{2,1,0:T(8,128)(2,1)}, bf16[1,136,128]{2,1,0:T(8,128)(2,1)S(1)}, u32[]{:S(2)}, u32[]{:S(2)}) collective-permute-start(bf16[1,136,128]{2,1,0:T(8,128)(2,1)} %get-tuple-element.21), channel_id=1, source_target_pairs={{0,16},{1,17},{2,18},{3,19},{4,20},{5,21},{6,22},{7,23},{8,24},{9,... | collective-permute-start | bytes 104456 | tf_op jit(solution)/shard_map/ppermute | solution.py:425
  30.3 15.5 %collective-permute-start.3 = (bf16[1,136,128]{2,1,0:T(8,128)(2,1)}, bf16[1,136,128]{2,1,0:T(8,128)(2,1)S(1)}, u32[]{:S(2)}, u32[]{:S(2)}) collective-permute-start(bf16[1,136,128]{2,1,0:T(8,128)(2,1)} %get-tuple-element.22), channel_id=1, source_target_pairs={{0,17},{1,16},{2,19},{3,18},{4,21},{5,20},{6,23},{7,22},{8,25},{9,... | collective-permute-start | bytes 104456 | tf_op jit(solution)/shard_map/ppermute | solution.py:425
  30.3 15.5 %collective-permute-start.4 = (bf16[1,136,128]{2,1,0:T(8,128)(2,1)}, bf16[1,136,128]{2,1,0:T(8,128)(2,1)S(1)}, u32[]{:S(2)}, u32[]{:S(2)}) collective-permute-start(bf16[1,136,128]{2,1,0:T(8,128)(2,1)} %get-tuple-element.23), channel_id=1, source_target_pairs={{0,18},{1,19},{2,16},{3,17},{4,22},{5,23},{6,20},{7,21},{8,26},{9,... | collective-permute-start | bytes 104456 | tf_op jit(solution)/shard_map/ppermute | solution.py:425
  40.2 5.6 %collective-permute-start.5 = (bf16[1,136,128]{2,1,0:T(8,128)(2,1)}, bf16[1,136,128]{2,1,0:T(8,128)(2,1)S(1)}, u32[]{:S(2)}, u32[]{:S(2)}) collective-permute-start(bf16[1,136,128]{2,1,0:T(8,128)(2,1)} %get-tuple-element.24), channel_id=1, source_target_pairs={{0,19},{1,18},{2,17},{3,16},{4,23},{5,22},{6,21},{7,20},{8,27},{9,... | collective-permute-start | bytes 104456 | tf_op jit(solution)/shard_map/ppermute | solution.py:425
  40.3 0.8 %copy-start.5 = (f32[10240]{0:T(1024)S(1)}, f32[10240]{0:T(1024)}, u32[]{:S(2)}) copy-start(f32[10240]{0:T(1024)} %param.11) | copy-start | bytes 122884
  41.1 0.7 copy-start.7
  44.3 1.5 %copy-start.1 = (f32[20,256,128]{2,1,0:T(8,128)}, f32[20,256,128]{2,1,0:T(8,128)S(1)}, u32[]{:S(2)}) copy-start(f32[20,256,128]{2,1,0:T(8,128)S(1)} %get-tuple-element.27.accum_rep_ref) | copy-start | bytes 7864324
  55.7 1.5 %copy-start.3 = (f32[20,256,128]{2,1,0:T(8,128)}, f32[20,256,128]{2,1,0:T(8,128)S(1)}, u32[]{:S(2)}) copy-start(f32[20,256,128]{2,1,0:T(8,128)S(1)} %get-tuple-element.28.mean_rep_ref) | copy-start | bytes 7864324
  57.2 11.9 %all-to-all-start.1 = ((f32[16,8,128]{2,1,0:T(8,128)}), f32[16,8,128]{2,1,0:T(8,128)S(1)}, u32[]{:S(2)}, u32[]{:S(2)}) async-start(f32[16,8,128]{2,1,0:T(8,128)} %get-tuple-element.25), calls=%async_computation.1 | async-start | bytes 131072 | tf_op jit(solution)/shard_map/all_to_all | solution.py:403
  62.2 6.9 %copy-start.6 = (f32[10240]{0:T(1024)S(1)}, f32[10240]{0:T(1024)}, u32[]{:S(2)}) copy-start(f32[10240]{0:T(1024)} %param.11) | copy-start | bytes 122884
  62.2 6.9 %copy-start.8 = (s32[1,20]{1,0:T(1,128)S(1)}, s32[1,20]{1,0:T(1,128)}, u32[]{:S(2)}) copy-start(s32[1,20]{1,0:T(1,128)} %touched_hbm.5) | copy-start | bytes 244
  69.1 2.5 %copy-start = (f32[10240,128]{1,0:T(8,128)S(1)}, f32[10240,128]{1,0:T(8,128)}, u32[]{:S(2)}) copy-start(f32[10240,128]{1,0:T(8,128)} %param.10) | copy-start | bytes 15728644
  71.6 1.7 %copy-start.2 = (f32[20,256,128]{2,1,0:T(8,128)S(1)}, f32[20,256,128]{2,1,0:T(8,128)}, u32[]{:S(2)}) copy-start(f32[20,256,128]{2,1,0:T(8,128)} %copy-done.1) | copy-start | bytes 7864324
  73.3 1.7 %copy-start.4 = (f32[20,256,128]{2,1,0:T(8,128)S(1)}, f32[20,256,128]{2,1,0:T(8,128)}, u32[]{:S(2)}) copy-start(f32[20,256,128]{2,1,0:T(8,128)} %copy-done.3) | copy-start | bytes 7864324
